TPU v7x, 32 devices: a whole 2x2x4 slice. The times are simulated.
32 devices in a mesh: samp: 8 (over z, y), gene: 4 (over x, core).
Axes of the slice: x: 2, y: 2, z: 4, core: 2. Of those that a mesh axis runs over, the one named last changes fastest.
Arguments:
- genotypes: int32 [256, 4096], P('samp', 'gene'), may hold values from -2147483648 to 1789569706, as said below
- allele_freq: float32 [4096], P('gene'), may hold values from 0.035 to 0.56
- sample_weight: float32 [16, 256], P(None, 'samp'), may hold values from 0.2 to 2
- residual: float32 [16, 256], P(None, 'samp'), may hold values from -12 to 12
- variant_weight: float32 [4096], P('gene'), may hold values from 0.2 to 4
- block_gene: int32 [32], replicated, may hold values from 0 to 15, as said below
- gene_variants: int32 [16], replicated, may hold values from 1 to 384, as said below
Outputs:
- burden_z: float32 [16], replicated
- skat_z: float32 [16], replicated
Inputs may be any that keep to these rules, and one draw needn't show every extreme that they name: Each word holds 16 dosages 0, 1 or 2: bits 2k and 2k+1 of genotypes[i, v] are the dosage of variant slot v in sample (k, i); a dosage 2 in the top field sets the sign bit. `block_gene`: never falling; the blocks come in aligned groups of four, each shared by two consecutive genes, so every gene has 1 to 3 blocks. `gene_variants`: A gene with m blocks has from (m - 1) * 128 + 1 to m * 128 live variants; the slots after them in its last block are padding.
All inputs are finite; a program needn't handle non-finite values.
Results may differ from a plain program's by a relative error of at most 0.0037.
Values sent between devices are 32-bit elements; how exact they have to be, the bound alone decides.
A program may use at most 64 MiB of HBM per device.

v0:
```python
import functools

import jax
import jax.numpy as jnp
from jax import lax
from jax.experimental import pallas as pl
from jax.experimental.pallas import tpu as pltpu
from jax.sharding import PartitionSpec as P

BLK = 128
MESH = pl.DeviceIdType.MESH
STATS = 5


def lane_sum(row):
    return jnp.sum(row, axis=1, keepdims=True)


def kernel(
    samp_size,
    gene_size,
    genotypes_hbm,
    freq_hbm,
    weight_hbm,
    residual_hbm,
    variant_hbm,
    block_gene_hbm,
    counts_hbm,
    both_ref,
    words_in,
    freq_in,
    weight_in,
    residual_in,
    variant_in,
    block_gene_in,
    counts_in,
    tile_out,
    tiles,
    words,
    scaled,
    root_rows,
    residual_rows,
    power_rows,
    pair_weight,
    row_out,
    rows,
    load_sem,
    send_sem,
    tile_sem,
    word_sem,
    row_send_sem,
    row_sem,
    ready_sem,
    others_sem,
):
    devices = samp_size * gene_size
    samp = lax.axis_index("samp")
    gene = lax.axis_index("gene")
    me = samp * gene_size + gene
    fields, local_rows = weight_in.shape
    half = fields // 2
    group = BLK // local_rows
    chunks = samp_size // group
    owned = words.shape[1] // BLK
    local_blocks = freq_in.shape[0]
    genes = counts_in.shape[1]
    width = row_out.shape[1]

    loads = [
        pltpu.make_async_copy(source, target, load_sem.at[place])
        for place, (source, target) in enumerate(
            (
                (genotypes_hbm, words_in),
                (weight_hbm, weight_in),
                (residual_hbm, residual_in),
                (freq_hbm, freq_in),
                (variant_hbm, variant_in),
                (block_gene_hbm, block_gene_in),
                (counts_hbm, counts_in),
            )
        )
    ]
    for load in loads:
        load.start()

    def signal(semaphore, samp_to, gene_to):
        pl.semaphore_signal(
            semaphore,
            inc=1,
            device_id={"samp": samp_to, "gene": gene_to},
            device_id_type=MESH,
        )

    barrier = pltpu.get_barrier_semaphore()
    for gene_to in range(gene_size):

        @pl.when(gene_to > gene)
        def _(gene_to=gene_to):
            signal(barrier, samp, gene_to)

    @pl.loop(samp + 1, samp_size)
    def _(samp_to):
        for gene_to in range(gene_size):
            signal(barrier, samp_to, gene_to)

    loads[1].wait()
    loads[2].wait()
    own_weight, own_residual = weight_in[...], residual_in[...]
    own_tile = jnp.concatenate(
        [own_weight[:half], own_weight[half:], own_residual[:half], own_residual[half:]], axis=1
    )
    tile_out[...] = own_tile
    tiles[samp] = own_tile

    @pl.when(me > 0)
    def _():
        pl.semaphore_wait(barrier, me)

    @pl.loop(0, samp)
    def _(samp_to):
        signal(ready_sem.at[samp], samp_to, gene)

    def tile_copy(peer, slot):
        return pltpu.make_async_remote_copy(
            src_ref=tile_out,
            dst_ref=tiles.at[samp],
            send_sem=send_sem.at[0],
            recv_sem=tile_sem.at[slot],
            device_id={"samp": peer, "gene": gene},
            device_id_type=MESH,
        )

    def word_copy(peer, slot):
        start = pl.multiple_of(peer * (owned * BLK), BLK)
        return pltpu.make_async_remote_copy(
            src_ref=words_in.at[:, pl.ds(start, owned * BLK)],
            dst_ref=words.at[pl.ds(pl.multiple_of(samp * local_rows, local_rows), local_rows), :],
            send_sem=send_sem.at[1],
            recv_sem=word_sem.at[slot],
            device_id={"samp": peer, "gene": gene},
            device_id_type=MESH,
        )

    @pl.loop(0, samp)
    def _(peer):
        tile_copy(peer, samp).start()

    loads[0].wait()

    @pl.loop(0, samp)
    def _(peer):
        word_copy(peer, samp).start()

    for gene_to in range(gene_size):

        @pl.when(gene_to < gene)
        def _(gene_to=gene_to):
            signal(others_sem, samp, gene_to)

        @pl.when(gene_to != gene)
        def _(gene_to=gene_to):
            @pl.loop(0, samp)
            def _(samp_to):
                signal(others_sem, samp_to, gene_to)

    own_start = pl.multiple_of(samp * (owned * BLK), BLK)
    own_place = pl.multiple_of(samp * local_rows, local_rows)
    words[pl.ds(own_place, local_rows), :] = words_in[:, pl.ds(own_start, owned * BLK)]

    for load in loads[3:]:
        load.wait()
    block_gene = block_gene_in[...].astype(jnp.float32)
    counts = counts_in[...].astype(jnp.float32)
    block_lane = lax.broadcasted_iota(jnp.int32, block_gene.shape, 1)
    gene_lane = lax.broadcasted_iota(jnp.int32, counts.shape, 1).astype(jnp.float32)
    column = lax.broadcasted_iota(jnp.int32, (1, BLK), 1).astype(jnp.float32)
    stat_sub = lax.broadcasted_iota(jnp.int32, (8, width), 0)
    stat_lane = lax.broadcasted_iota(jnp.int32, (8, width), 1) - stat_sub * genes
    effective, places, twice = [], [], []
    for block in range(owned):
        local_block = samp * owned + block
        block_id = gene * local_blocks + local_block
        gene_of = lane_sum(jnp.where(block_lane == block_id, block_gene, 0.0))
        first = lane_sum(jnp.where(block_gene < gene_of, 1.0, 0.0))
        counted = lane_sum(jnp.where(gene_lane == gene_of, counts, 0.0))
        block_float = jnp.zeros((1, 1), jnp.float32) + block_id.astype(jnp.float32)
        live = (block_float - first) * BLK + column < counted
        weights = jnp.where(live, variant_in[pl.ds(local_block, 1), :], 0.0)
        effective.append(weights)
        across = jnp.broadcast_to(weights, (BLK, BLK))
        pair_weight[block] = across * across.T
        twice.append(2.0 * jnp.broadcast_to(freq_in[pl.ds(local_block, 1), :], (BLK, BLK)).T)
        member = stat_lane.astype(jnp.float32) == gene_of
        places.append(jnp.where(member & (stat_sub < STATS), 1.0, 0.0))

    def wait_tile(peer):
        pltpu.make_async_copy(tile_out, tiles.at[peer], tile_sem.at[peer]).wait()

    def wait_words(peer):
        place = words.at[pl.ds(pl.multiple_of(peer * local_rows, local_rows), local_rows), :]
        pltpu.make_async_copy(place, place, word_sem.at[peer]).wait()

    @pl.loop(samp + 1, samp_size)
    def _(peer):
        pl.semaphore_wait(ready_sem.at[peer], 1)
        tile_copy(peer, samp).start()
        word_copy(peer, samp).start()

    own_chunk = lax.div(samp, group)

    def add_chunk(step, totals):
        chunk = lax.rem(own_chunk + step, chunks)
        for place in range(group):

            @pl.when(chunk * group + place != samp)
            def _(peer=chunk * group + place):
                wait_tile(peer)

        parts = [tiles[chunk * group + place] for place in range(group)]
        kinds = [
            jnp.concatenate(
                [part[:, kind * local_rows : (kind + 1) * local_rows] for part in parts], axis=1
            )
            for kind in range(4)
        ]
        power = jnp.zeros((half, BLK), jnp.float32)
        for upper in range(2):
            weight, resid = kinds[upper], kinds[2 + upper]
            root = jnp.sqrt(weight)
            power = power + weight * resid * resid
            root_rows[upper * half : (upper + 1) * half, :] = root
            residual_rows[upper * half : (upper + 1) * half, :] = root * resid
        power_rows[chunk] = power
        for place in range(group):

            @pl.when(chunk * group + place != samp)
            def _(peer=chunk * group + place):
                wait_words(peer)

        start = pl.multiple_of(chunk * BLK, BLK)
        results = []
        for block in range(owned):
            turned = words[pl.ds(start, BLK), block * BLK : (block + 1) * BLK].T
            for field in range(fields):
                dosage = jnp.bitwise_and(jnp.right_shift(turned, 2 * field), 3)
                root = root_rows[field : field + 1, :]
                value = (root * (dosage.astype(jnp.float32) - twice[block])).astype(jnp.bfloat16)
                score = residual_rows[field : field + 1, :]
                lanes = slice(field * BLK, (field + 1) * BLK)
                scaled[:BLK, lanes] = value
                scaled[BLK:, lanes] = jnp.broadcast_to(score, (16, BLK)).astype(jnp.bfloat16)
            results.append(
                totals[block]
                + lax.dot_general(
                    scaled[...],
                    scaled[:BLK, :],
                    (((1,), (1,)), ((), ())),
                    preferred_element_type=jnp.float32,
                )
            )
        return tuple(results)

    totals = tuple(jnp.zeros((BLK + 16, BLK), jnp.float32) for _ in range(owned))
    if chunks <= 2:
        for step in range(chunks):
            totals = add_chunk(step, totals)
    else:
        totals = lax.fori_loop(0, chunks, add_chunk, totals)

    message = jnp.zeros((8, width), jnp.float32)
    diagonal = lax.broadcasted_iota(jnp.int32, (BLK, BLK), 0) == lax.broadcasted_iota(
        jnp.int32, (BLK, BLK), 1
    )
    for block in range(owned):
        total = totals[block]
        weighted = total[:BLK] * pair_weight[block]
        score = effective[block] * total[BLK : BLK + 1]
        sums = [
            score,
            jnp.sum(weighted, axis=0, keepdims=True),
            score * score,
            jnp.sum(jnp.where(diagonal, weighted, 0.0), axis=0, keepdims=True),
            jnp.sum(weighted * weighted, axis=0, keepdims=True),
            jnp.zeros((8 - STATS, BLK), jnp.float32),
        ]
        message = message + lane_sum(jnp.concatenate(sums, axis=0)) * places[block]
    row = jnp.sum(message, axis=0, keepdims=True)
    others = (samp_size - 1 - samp) * (gene_size - 1) + gene_size - 1 - gene

    @pl.when(others > 0)
    def _():
        pl.semaphore_wait(others_sem, others)

    row_out[...] = row
    rows[me] = row

    def row_copy(samp_to, gene_to):
        return pltpu.make_async_remote_copy(
            src_ref=row_out,
            dst_ref=rows.at[me],
            send_sem=row_send_sem,
            recv_sem=row_sem,
            device_id={"samp": samp_to, "gene": gene_to},
            device_id_type=MESH,
        )

    @pl.loop(1, samp_size)
    def _(step):
        gap = samp_size - step

        @pl.when(samp + gap < samp_size)
        def _():
            for gene_to in range(gene_size):
                row_copy(samp + gap, gene_to).start()

        @pl.when(samp - gap >= 0)
        def _():
            for gene_to in range(gene_size):
                row_copy(samp - gap, gene_to).start()

    for gene_to in range(gene_size):

        @pl.when(gene_to != gene)
        def _(gene_to=gene_to):
            row_copy(samp, gene_to).start()

    power = jnp.sum(power_rows[...], axis=0)
    variance = lane_sum(jnp.sum(power, axis=0, keepdims=True)) / (
        fields * local_rows * samp_size
    )
    landed = rows.at[pl.ds(0, devices - 1)]
    pltpu.make_async_copy(landed, landed, row_sem).wait()
    totals = jnp.sum(rows[...], axis=0)
    parts = [totals[:, stat * genes : (stat + 1) * genes] for stat in range(STATS)]
    both_ref[0:1] = parts[0] / jnp.sqrt(variance * parts[1])
    both_ref[1:2] = (parts[2] - variance * parts[3]) / (
        variance * jnp.sqrt(2.0 * parts[4])
    )

    pltpu.make_async_copy(landed, landed, row_send_sem).wait()

    sent_tiles = tiles.at[pl.ds(0, samp_size - 1)]
    pltpu.make_async_copy(sent_tiles, sent_tiles, send_sem.at[0]).wait()
    sent_words = words.at[pl.ds(0, (samp_size - 1) * local_rows), :]
    pltpu.make_async_copy(sent_words, sent_words, send_sem.at[1]).wait()


def solution(mesh):
    samp_size, gene_size = mesh.shape["samp"], mesh.shape["gene"]
    devices = samp_size * gene_size

    def local(
        genotypes, allele_freq, sample_weight, residual, variant_weight, block_gene, gene_variants
    ):
        local_rows, columns = genotypes.shape
        local_blocks = columns // BLK
        owned = local_blocks // samp_size
        fields = sample_weight.shape[0]
        genes = gene_variants.shape[0]
        width = -(-STATS * genes // BLK) * BLK
        chunks = samp_size * local_rows // BLK
        both = pl.pallas_call(
            functools.partial(kernel, samp_size, gene_size),
            out_shape=pltpu.VMEM((2, genes), jnp.float32),
            in_specs=[pl.BlockSpec(memory_space=pl.ANY)] * 7,
            out_specs=pl.BlockSpec(memory_space=pltpu.VMEM),
            scratch_shapes=[
                pltpu.VMEM((local_rows, columns), jnp.int32),
                pltpu.VMEM((local_blocks, BLK), jnp.float32),
                pltpu.VMEM((fields, local_rows), jnp.float32),
                pltpu.VMEM((fields, local_rows), jnp.float32),
                pltpu.VMEM((local_blocks, BLK), jnp.float32),
                pltpu.VMEM((1, block_gene.shape[0]), jnp.int32),
                pltpu.VMEM((1, genes), jnp.int32),
                pltpu.VMEM((fields // 2, 4 * local_rows), jnp.float32),
                pltpu.VMEM((samp_size, fields // 2, 4 * local_rows), jnp.float32),
                pltpu.VMEM((samp_size * local_rows, owned * BLK), jnp.int32),
                pltpu.VMEM((BLK + 16, fields * BLK), jnp.bfloat16),
                pltpu.VMEM((fields, BLK), jnp.float32),
                pltpu.VMEM((fields, BLK), jnp.float32),
                pltpu.VMEM((chunks, fields // 2, BLK), jnp.float32),
                pltpu.VMEM((owned, BLK, BLK), jnp.float32),
                pltpu.VMEM((1, width), jnp.float32),
                pltpu.VMEM((devices, 1, width), jnp.float32),
                pltpu.SemaphoreType.DMA((7,)),
                pltpu.SemaphoreType.DMA((2,)),
                pltpu.SemaphoreType.DMA((samp_size,)),
                pltpu.SemaphoreType.DMA((samp_size,)),
                pltpu.SemaphoreType.DMA,
                pltpu.SemaphoreType.DMA,
                pltpu.SemaphoreType.REGULAR((samp_size,)),
                pltpu.SemaphoreType.REGULAR,
            ],
            compiler_params=pltpu.CompilerParams(collective_id=0, has_side_effects=True),
        )(
            genotypes,
            allele_freq.reshape(local_blocks, BLK),
            sample_weight,
            residual,
            variant_weight.reshape(local_blocks, BLK),
            block_gene.reshape(1, -1),
            gene_variants.reshape(1, -1),
        )
        return both[0], both[1]

    placed = (P("samp", "gene"), P("gene"), P(None, "samp"), P(None, "samp"), P("gene"), P(), P())
    return jax.shard_map(local, mesh=mesh, in_specs=placed, out_specs=(P(), P()), check_vma=False)
```

profile of v0, /device:TPU:0, one launch (start us, length us, event | category | flops | bytes accessed | tf_op | source)
XLA Modules:
  0.0 18.8 jit_solution(2864466939183314457)
XLA Ops:
  0.6 17.6 %shard_map.86 = f32[2,16]{1,0:T(2,128)S(1)} custom-call(s32[32,1024]{1,0:T(8,128)} %genotypes_hbm.1, f32[8,128]{1,0:T(8,128)} %bitcast.8, f32[16,32]{1,0:T(8,128)} %weight_hbm.1, f32[16,32]{1,0:T(8,128)} %residual_hbm.1, f32[8,128]{1,0:T(8,128)} %bitcast.9, s32[1,32]{1,0:T(1,128)} %bitcast.10, s32[1,16]{1,0:T(1,128)} %bitcast.11), custom_call_target="tpu_custom_call" | custom-call | tf_op jit(solution)/shard_map/pallas_call | solution.py:362
  18.3 0.5 %slice_bitcast_fusion = (f32[16]{0:T(128)}, f32[16]{0:T(128)}) fusion(f32[2,16]{1,0:T(2,128)S(1)} %shard_map.86), kind=kLoop, calls=%fused_computation | loop fusion | bytes 256 | tf_op jit(solution)/shard_map/squeeze | solution.py:404
where the time goes:
time: 18.9 us; the launch traced here: 18.8 us
  Pallas kernels  17.6 us (93%)
  between operations  0.64 us (3%)
  local copies, waits for them, and re-layouts  0.52 us (3%)
    pallas_call x1, Pallas kernels, local(): pl.pallas_call(functools.partial(kernel, samp_size, gene_size), out_shape...  17.6 us
    squeeze x1, local copies, waits for them, and re-layouts, local(): return (both[0], both[1])  0.52 us

commit v1 on v0

v1 whole, which is shorter than its diff:
```python
import functools

import jax
import jax.numpy as jnp
from jax import lax
from jax.experimental import pallas as pl
from jax.experimental.pallas import tpu as pltpu
from jax.sharding import PartitionSpec as P

BLK = 128
MESH = pl.DeviceIdType.MESH
STATS = 5
SCORE = 16


def lane_sum(row):
    return jnp.sum(row, axis=1, keepdims=True)


def owner_range(samp_size, local_blocks):
    low = samp_size // 4
    size = max(1, samp_size // 2)
    while local_blocks % size:
        size -= 1
    return low, size


def flip(samp, step):
    peer, bit = samp, 1
    while bit <= step:
        if step & bit:
            peer = peer + bit * (1 - 2 * lax.rem(lax.div(samp, bit), 2))
        bit *= 2
    return peer


def kernel(
    samp_size,
    gene_size,
    owner_low,
    owner_size,
    genotypes_hbm,
    freq_hbm,
    weight_hbm,
    residual_hbm,
    variant_hbm,
    block_gene_hbm,
    counts_hbm,
    both_ref,
    words_in,
    freq_in,
    weight_in,
    residual_in,
    variant_in,
    block_gene_in,
    counts_in,
    tile_out,
    tiles,
    words,
    scaled,
    centers,
    pair_weight,
    row_out,
    rows,
    load_sem,
    send_sem,
    tile_sem,
    word_sem,
    row_send_sem,
    row_sem,
    ready_sem,
    others_sem,
):
    samp = lax.axis_index("samp")
    gene = lax.axis_index("gene")
    me = samp * gene_size + gene
    fields, local_rows = weight_in.shape
    group = BLK // local_rows
    depth = fields // group
    local_blocks = freq_in.shape[0]
    owned = local_blocks // owner_size
    owner_high = owner_low + owner_size
    genes = counts_in.shape[1]
    width = row_out.shape[1]
    owns = jnp.logical_and(samp >= owner_low, samp < owner_high)
    place = samp - owner_low

    loads = [
        pltpu.make_async_copy(source, target, load_sem.at[number])
        for number, (source, target) in enumerate(
            (
                (genotypes_hbm, words_in),
                (weight_hbm, weight_in),
                (residual_hbm, residual_in),
                (freq_hbm, freq_in),
                (variant_hbm, variant_in),
                (block_gene_hbm, block_gene_in),
                (counts_hbm, counts_in),
            )
        )
    ]
    for load in loads:
        load.start()

    def signal(semaphore, samp_to, gene_to):
        pl.semaphore_signal(
            semaphore,
            inc=1,
            device_id={"samp": samp_to, "gene": gene_to},
            device_id_type=MESH,
        )

    barrier = pltpu.get_barrier_semaphore()
    for gene_to in range(gene_size):

        @pl.when(jnp.logical_and(owns, gene_to > gene))
        def _(gene_to=gene_to):
            signal(barrier, samp, gene_to)

    first_to = jnp.where(owns, samp + 1, jnp.maximum(samp + 1, owner_low))
    last_to = jnp.where(owns, samp_size, owner_high)

    @pl.loop(first_to, last_to)
    def _(samp_to):
        for gene_to in range(gene_size):
            signal(barrier, samp_to, gene_to)

    loads[1].wait()
    loads[2].wait()
    own_weight, own_residual = weight_in[...], residual_in[...]
    own_tile = jnp.concatenate(
        [
            jnp.concatenate(
                [part[lanes * depth : (lanes + 1) * depth] for lanes in range(group)], axis=1
            )
            for part in (own_weight, own_residual)
        ],
        axis=0,
    )
    tile_out[...] = own_tile
    tiles[samp] = own_tile

    earlier_owners = jnp.clip(samp - owner_low, 0, owner_size)
    greeted = jnp.where(owns, me, earlier_owners * gene_size)

    @pl.when(greeted > 0)
    def _():
        pl.semaphore_wait(barrier, greeted)

    @pl.when(owns)
    def _():
        @pl.loop(0, samp)
        def _(samp_to):
            signal(ready_sem.at[place], samp_to, gene)

    def tile_copy(owner):
        return pltpu.make_async_remote_copy(
            src_ref=tile_out,
            dst_ref=tiles.at[samp],
            send_sem=send_sem.at[0],
            recv_sem=tile_sem.at[samp],
            device_id={"samp": owner, "gene": gene},
            device_id_type=MESH,
        )

    def word_copy(owner):
        start = pl.multiple_of((owner - owner_low) * (owned * BLK), BLK)
        return pltpu.make_async_remote_copy(
            src_ref=words_in.at[:, pl.ds(start, owned * BLK)],
            dst_ref=words.at[samp],
            send_sem=send_sem.at[1],
            recv_sem=word_sem.at[samp],
            device_id={"samp": owner, "gene": gene},
            device_id_type=MESH,
        )

    earlier = jnp.minimum(samp, owner_high)

    @pl.loop(owner_low, earlier)
    def _(owner):
        tile_copy(owner).start()

    loads[0].wait()

    @pl.loop(owner_low, earlier)
    def _(owner):
        word_copy(owner).start()

    for gene_to in range(gene_size):

        @pl.when(jnp.logical_and(owns, gene_to < gene))
        def _(gene_to=gene_to):
            signal(others_sem, samp, gene_to)

        @pl.when(gene_to != gene)
        def _(gene_to=gene_to):
            @pl.loop(owner_low, earlier)
            def _(samp_to):
                signal(others_sem, samp_to, gene_to)

    @pl.loop(jnp.maximum(samp + 1, owner_low), owner_high)
    def _(owner):
        pl.semaphore_wait(ready_sem.at[owner - owner_low], 1)
        tile_copy(owner).start()
        word_copy(owner).start()

    for load in loads[3:]:
        load.wait()

    @pl.when(owns)
    def _():
        own_start = pl.multiple_of(place * (owned * BLK), BLK)
        words[samp] = words_in[:, pl.ds(own_start, owned * BLK)]
        block_gene = block_gene_in[...].astype(jnp.float32)
        counts = counts_in[...].astype(jnp.float32)
        block_lane = lax.broadcasted_iota(jnp.int32, block_gene.shape, 1)
        gene_lane = lax.broadcasted_iota(jnp.int32, counts.shape, 1).astype(jnp.float32)
        column = lax.broadcasted_iota(jnp.int32, (1, BLK), 1).astype(jnp.float32)
        stat_sub = lax.broadcasted_iota(jnp.int32, (8, width), 0)
        stat_lane = lax.broadcasted_iota(jnp.int32, (8, width), 1) - stat_sub * genes
        effective, places = [], []
        for block in range(owned):
            local_block = place * owned + block
            block_id = gene * local_blocks + local_block
            gene_of = lane_sum(jnp.where(block_lane == block_id, block_gene, 0.0))
            first = lane_sum(jnp.where(block_gene < gene_of, 1.0, 0.0))
            counted = lane_sum(jnp.where(gene_lane == gene_of, counts, 0.0))
            block_float = jnp.zeros((1, 1), jnp.float32) + block_id.astype(jnp.float32)
            live = (block_float - first) * BLK + column < counted
            weights = jnp.where(live, variant_in[pl.ds(local_block, 1), :], 0.0)
            effective.append(weights)
            across = jnp.broadcast_to(weights, (BLK, BLK))
            pair_weight[block] = across * across.T
            center = 2.0 * jnp.broadcast_to(freq_in[pl.ds(local_block, 1), :], (BLK, BLK)).T
            for level in range(depth):
                centers[block, level] = center * float(4**level)
            member = stat_lane.astype(jnp.float32) == gene_of
            places.append(jnp.where(member & (stat_sub < STATS), 1.0, 0.0))

        def add_peer(peer, totals, power):
            @pl.when(peer != samp)
            def _():
                pltpu.make_async_copy(tile_out, tiles.at[peer], tile_sem.at[peer]).wait()

            tile = tiles[peer]
            weight, resid = tile[:depth], tile[depth:]
            root = jnp.sqrt(weight)
            score = root * resid
            power = power + weight * resid * resid

            @pl.when(peer != samp)
            def _():
                landed = words.at[peer]
                pltpu.make_async_copy(landed, landed, word_sem.at[peer]).wait()

            results = []
            for block in range(owned):
                part = words[peer, :, block * BLK : (block + 1) * BLK]
                turned = jnp.concatenate(
                    [lax.shift_right_logical(part, 2 * depth * lanes) for lanes in range(group)],
                    axis=0,
                ).T
                for level in range(depth):
                    dosage = jnp.bitwise_and(turned, 3 << (2 * level)).astype(jnp.float32)
                    scale = root[level : level + 1] * float(4**-level)
                    lanes = slice(level * BLK, (level + 1) * BLK)
                    scaled[block, :BLK, lanes] = (
                        (dosage - centers[block, level]) * scale
                    ).astype(jnp.bfloat16)
                    scaled[block, BLK:, lanes] = jnp.broadcast_to(
                        score[level : level + 1], (SCORE, BLK)
                    ).astype(jnp.bfloat16)
                results.append(
                    totals[block]
                    + lax.dot_general(
                        scaled[block],
                        scaled[block, :BLK],
                        (((1,), (1,)), ((), ())),
                        preferred_element_type=jnp.float32,
                    )
                )
            return tuple(results), power

        totals = tuple(jnp.zeros((BLK + SCORE, BLK), jnp.float32) for _ in range(owned))
        power = jnp.zeros((depth, BLK), jnp.float32)
        if samp_size == 8:
            for step in (0, 1, 2, 3, 6, 7, 4, 5):
                totals, power = add_peer(flip(samp, step), totals, power)
        else:
            totals, power = lax.fori_loop(
                0,
                samp_size,
                lambda step, carry: add_peer(lax.rem(samp + step, samp_size), *carry),
                (totals, power),
            )

        message = jnp.zeros((8, width), jnp.float32)
        diagonal = lax.broadcasted_iota(jnp.int32, (BLK, BLK), 0) == lax.broadcasted_iota(
            jnp.int32, (BLK, BLK), 1
        )
        for block in range(owned):
            total = totals[block]
            weighted = total[:BLK] * pair_weight[block]
            score = effective[block] * total[BLK : BLK + 1]
            sums = [
                score,
                jnp.sum(weighted, axis=0, keepdims=True),
                score * score,
                jnp.sum(jnp.where(diagonal, weighted, 0.0), axis=0, keepdims=True),
                jnp.sum(weighted * weighted, axis=0, keepdims=True),
                jnp.zeros((8 - STATS, BLK), jnp.float32),
            ]
            message = message + lane_sum(jnp.concatenate(sums, axis=0)) * places[block]
        squares = lane_sum(jnp.sum(power, axis=0, keepdims=True))
        lane = lax.broadcasted_iota(jnp.int32, (1, width), 1)
        reports = jnp.logical_and(place == 0, gene == 0).astype(jnp.float32)
        row = jnp.sum(message, axis=0, keepdims=True) + jnp.where(
            lane == STATS * genes, squares * reports, 0.0
        )

        others = (samp_size - 1 - samp) * (gene_size - 1) + gene_size - 1 - gene

        @pl.when(others > 0)
        def _():
            pl.semaphore_wait(others_sem, others)

        row_out[...] = row
        slot = place * gene_size + gene
        rows[slot] = row

        @pl.loop(0, samp_size)
        def _(samp_to):
            for gene_to in range(gene_size):

                @pl.when(jnp.logical_or(samp_to != samp, gene_to != gene))
                def _(gene_to=gene_to):
                    pltpu.make_async_remote_copy(
                        src_ref=row_out,
                        dst_ref=rows.at[slot],
                        send_sem=row_send_sem,
                        recv_sem=row_sem,
                        device_id={"samp": samp_to, "gene": gene_to},
                        device_id_type=MESH,
                    ).start()

    row_count = owner_size * gene_size

    @pl.when(owns)
    def _():
        landed = rows.at[pl.ds(0, row_count - 1)]
        pltpu.make_async_copy(landed, landed, row_sem).wait()

    @pl.when(jnp.logical_not(owns))
    def _():
        pltpu.make_async_copy(rows, rows, row_sem).wait()

    totals = jnp.sum(rows[...], axis=0)
    parts = [totals[:, stat * genes : (stat + 1) * genes] for stat in range(STATS)]
    variance = totals[:, STATS * genes : STATS * genes + 1] / (fields * local_rows * samp_size)
    both_ref[0:1] = parts[0] / jnp.sqrt(variance * parts[1])
    both_ref[1:2] = (parts[2] - variance * parts[3]) / (
        variance * jnp.sqrt(2.0 * parts[4])
    )

    @pl.when(owns)
    def _():
        devices = samp_size * gene_size

        @pl.loop(0, devices - 1)
        def _(_):
            pltpu.make_async_copy(row_out, row_out, row_send_sem).wait()

    @pl.loop(0, jnp.where(owns, owner_size - 1, owner_size))
    def _(_):
        pltpu.make_async_copy(tile_out, tile_out, send_sem.at[0]).wait()
        pltpu.make_async_copy(words.at[0], words.at[0], send_sem.at[1]).wait()


def solution(mesh):
    samp_size, gene_size = mesh.shape["samp"], mesh.shape["gene"]

    def local(
        genotypes, allele_freq, sample_weight, residual, variant_weight, block_gene, gene_variants
    ):
        local_rows, columns = genotypes.shape
        local_blocks = columns // BLK
        fields = sample_weight.shape[0]
        genes = gene_variants.shape[0]
        depth = fields * local_rows // BLK
        width = -(-(STATS * genes + 1) // BLK) * BLK
        owner_low, owner_size = owner_range(samp_size, local_blocks)
        owned = local_blocks // owner_size
        both = pl.pallas_call(
            functools.partial(kernel, samp_size, gene_size, owner_low, owner_size),
            out_shape=pltpu.VMEM((2, genes), jnp.float32),
            in_specs=[pl.BlockSpec(memory_space=pl.ANY)] * 7,
            out_specs=pl.BlockSpec(memory_space=pltpu.VMEM),
            scratch_shapes=[
                pltpu.VMEM((local_rows, columns), jnp.int32),
                pltpu.VMEM((local_blocks, BLK), jnp.float32),
                pltpu.VMEM((fields, local_rows), jnp.float32),
                pltpu.VMEM((fields, local_rows), jnp.float32),
                pltpu.VMEM((local_blocks, BLK), jnp.float32),
                pltpu.VMEM((1, block_gene.shape[0]), jnp.int32),
                pltpu.VMEM((1, genes), jnp.int32),
                pltpu.VMEM((2 * depth, BLK), jnp.float32),
                pltpu.VMEM((samp_size, 2 * depth, BLK), jnp.float32),
                pltpu.VMEM((samp_size, local_rows, owned * BLK), jnp.int32),
                pltpu.VMEM((owned, BLK + SCORE, depth * BLK), jnp.bfloat16),
                pltpu.VMEM((owned, depth, BLK, BLK), jnp.float32),
                pltpu.VMEM((owned, BLK, BLK), jnp.float32),
                pltpu.VMEM((1, width), jnp.float32),
                pltpu.VMEM((owner_size * gene_size, 1, width), jnp.float32),
                pltpu.SemaphoreType.DMA((7,)),
                pltpu.SemaphoreType.DMA((2,)),
                pltpu.SemaphoreType.DMA((samp_size,)),
                pltpu.SemaphoreType.DMA((samp_size,)),
                pltpu.SemaphoreType.DMA,
                pltpu.SemaphoreType.DMA,
                pltpu.SemaphoreType.REGULAR((owner_size,)),
                pltpu.SemaphoreType.REGULAR,
            ],
            compiler_params=pltpu.CompilerParams(collective_id=0, has_side_effects=True),
        )(
            genotypes,
            allele_freq.reshape(local_blocks, BLK),
            sample_weight,
            residual,
            variant_weight.reshape(local_blocks, BLK),
            block_gene.reshape(1, -1),
            gene_variants.reshape(1, -1),
        )
        return both[0], both[1]

    placed = (P("samp", "gene"), P("gene"), P(None, "samp"), P(None, "samp"), P("gene"), P(), P())
    return jax.shard_map(local, mesh=mesh, in_specs=placed, out_specs=(P(), P()), check_vma=False)
```

time: 18.9 us -> 18.4 us (0.974)
  Pallas kernels: 17.6 us -> 17.1 us
    pallas_call x1, Pallas kernels: 17.6 us -> 17.1 us  [local(): pl.pallas_call(functools.partial(kernel, samp_size, gene_size, owner_low,...]
where the time goes in v1:
time: 18.4 us; the launch traced here: 18.2 us
  Pallas kernels  17.1 us (93%)
  between operations  0.64 us (3%)
  local copies, waits for them, and re-layouts  0.52 us (3%)
    pallas_call x1, Pallas kernels, local(): pl.pallas_call(functools.partial(kernel, samp_size, gene_size, owner_low,...  17.1 us
    squeeze x1, local copies, waits for them, and re-layouts, local(): return (both[0], both[1])  0.52 us

profile of v1, /device:TPU:0, one launch (start us, length us, event | category | flops | bytes accessed | tf_op | source)
XLA Modules:
  0.0 18.2 jit_solution(12738055882567880719)
XLA Ops:
  0.6 17.1 %shard_map.86 = f32[2,16]{1,0:T(2,128)S(1)} custom-call(s32[32,1024]{1,0:T(8,128)} %genotypes_hbm.1, f32[8,128]{1,0:T(8,128)} %bitcast.8, f32[16,32]{1,0:T(8,128)} %weight_hbm.1, f32[16,32]{1,0:T(8,128)} %residual_hbm.1, f32[8,128]{1,0:T(8,128)} %bitcast.9, s32[1,32]{1,0:T(1,128)} %bitcast.10, s32[1,16]{1,0:T(1,128)} %bitcast.11), custom_call_target="tpu_custom_call" | custom-call | tf_op jit(solution)/shard_map/pallas_call | solution.py:393
  17.7 0.5 %slice_bitcast_fusion = (f32[16]{0:T(128)}, f32[16]{0:T(128)}) fusion(f32[2,16]{1,0:T(2,128)S(1)} %shard_map.86), kind=kLoop, calls=%fused_computation | loop fusion | bytes 256 | tf_op jit(solution)/shard_map/squeeze | solution.py:433

commit v2 on v1

--- a/solution.py
+++ b/solution.py
@@ -68,8 +68,6 @@
     word_sem,
     row_send_sem,
     row_sem,
-    ready_sem,
-    others_sem,
 ):
     samp = lax.axis_index("samp")
     gene = lax.axis_index("gene")
@@ -84,6 +82,7 @@
     width = row_out.shape[1]
     owns = jnp.logical_and(samp >= owner_low, samp < owner_high)
     place = samp - owner_low
+    row_count = owner_size * gene_size
 
     loads = [
         pltpu.make_async_copy(source, target, load_sem.at[number])
@@ -111,19 +110,15 @@
         )
 
     barrier = pltpu.get_barrier_semaphore()
-    for gene_to in range(gene_size):
-
-        @pl.when(jnp.logical_and(owns, gene_to > gene))
-        def _(gene_to=gene_to):
-            signal(barrier, samp, gene_to)
-
-    first_to = jnp.where(owns, samp + 1, jnp.maximum(samp + 1, owner_low))
-    last_to = jnp.where(owns, samp_size, owner_high)
-
-    @pl.loop(first_to, last_to)
-    def _(samp_to):
-        for gene_to in range(gene_size):
-            signal(barrier, samp_to, gene_to)
+
+    @pl.when(owns)
+    def _():
+        @pl.loop(1, samp_size)
+        def _(step):
+            signal(barrier, lax.rem(samp + step, samp_size), gene)
+
+    for step in range(1, gene_size):
+        signal(barrier, samp, lax.rem(gene + step, gene_size))
 
     loads[1].wait()
     loads[2].wait()
@@ -140,18 +135,7 @@
     tile_out[...] = own_tile
     tiles[samp] = own_tile
 
-    earlier_owners = jnp.clip(samp - owner_low, 0, owner_size)
-    greeted = jnp.where(owns, me, earlier_owners * gene_size)
-
-    @pl.when(greeted > 0)
-    def _():
-        pl.semaphore_wait(barrier, greeted)
-
-    @pl.when(owns)
-    def _():
-        @pl.loop(0, samp)
-        def _(samp_to):
-            signal(ready_sem.at[place], samp_to, gene)
+    pl.semaphore_wait(barrier, jnp.where(owns, owner_size - 1, owner_size) + gene_size - 1)
 
     def tile_copy(owner):
         return pltpu.make_async_remote_copy(
@@ -174,35 +158,19 @@
             device_id_type=MESH,
         )
 
-    earlier = jnp.minimum(samp, owner_high)
-
-    @pl.loop(owner_low, earlier)
-    def _(owner):
-        tile_copy(owner).start()
-
+    upward = 2 * samp < 2 * owner_low + owner_size
+
+    def to_owners(send):
+        for order in range(owner_size):
+            owner = jnp.where(upward, owner_high - 1 - order, owner_low + order)
+
+            @pl.when(owner != samp)
+            def _(owner=owner):
+                send(owner).start()
+
+    to_owners(tile_copy)
     loads[0].wait()
-
-    @pl.loop(owner_low, earlier)
-    def _(owner):
-        word_copy(owner).start()
-
-    for gene_to in range(gene_size):
-
-        @pl.when(jnp.logical_and(owns, gene_to < gene))
-        def _(gene_to=gene_to):
-            signal(others_sem, samp, gene_to)
-
-        @pl.when(gene_to != gene)
-        def _(gene_to=gene_to):
-            @pl.loop(owner_low, earlier)
-            def _(samp_to):
-                signal(others_sem, samp_to, gene_to)
-
-    @pl.loop(jnp.maximum(samp + 1, owner_low), owner_high)
-    def _(owner):
-        pl.semaphore_wait(ready_sem.at[owner - owner_low], 1)
-        tile_copy(owner).start()
-        word_copy(owner).start()
+    to_owners(word_copy)
 
     for load in loads[3:]:
         load.wait()
@@ -284,7 +252,7 @@
         totals = tuple(jnp.zeros((BLK + SCORE, BLK), jnp.float32) for _ in range(owned))
         power = jnp.zeros((depth, BLK), jnp.float32)
         if samp_size == 8:
-            for step in (0, 1, 2, 3, 6, 7, 4, 5):
+            for step in (0, 1, 6, 7, 4, 5, 2, 3):
                 totals, power = add_peer(flip(samp, step), totals, power)
         else:
             totals, power = lax.fori_loop(
@@ -318,12 +286,6 @@
             lane == STATS * genes, squares * reports, 0.0
         )
 
-        others = (samp_size - 1 - samp) * (gene_size - 1) + gene_size - 1 - gene
-
-        @pl.when(others > 0)
-        def _():
-            pl.semaphore_wait(others_sem, others)
-
         row_out[...] = row
         slot = place * gene_size + gene
         rows[slot] = row
@@ -342,8 +304,6 @@
                         device_id={"samp": samp_to, "gene": gene_to},
                         device_id_type=MESH,
                     ).start()
-
-    row_count = owner_size * gene_size
 
     @pl.when(owns)
     def _():
@@ -417,8 +377,6 @@
                 pltpu.SemaphoreType.DMA((samp_size,)),
                 pltpu.SemaphoreType.DMA,
                 pltpu.SemaphoreType.DMA,
-                pltpu.SemaphoreType.REGULAR((owner_size,)),
-                pltpu.SemaphoreType.REGULAR,
             ],
             compiler_params=pltpu.CompilerParams(collective_id=0, has_side_effects=True),
         )(

time: 18.4 us -> 16.8 us (0.913)
  Pallas kernels: 17.1 us -> 15.5 us
    pallas_call x1, Pallas kernels: 17.1 us -> 15.5 us  [local(): pl.pallas_call(functools.partial(kernel, samp_size, gene_size, owner_low,...]
where the time goes in v2:
time: 16.8 us; the launch traced here: 16.7 us
  Pallas kernels  15.5 us (92%)
  between operations  0.64 us (4%)
  local copies, waits for them, and re-layouts  0.52 us (3%)
    pallas_call x1, Pallas kernels, local(): pl.pallas_call(functools.partial(kernel, samp_size, gene_size, owner_low,...  15.5 us
    squeeze x1, local copies, waits for them, and re-layouts, local(): return (both[0], both[1])  0.52 us

profile of v2, /device:TPU:0, one launch (start us, length us, event | category | flops | bytes accessed | tf_op | source)
XLA Modules:
  0.0 16.7 jit_solution(17299759626715170772)
XLA Ops:
  0.6 15.5 %shard_map.86 = f32[2,16]{1,0:T(2,128)S(1)} custom-call(s32[32,1024]{1,0:T(8,128)} %genotypes_hbm.1, f32[8,128]{1,0:T(8,128)} %bitcast.8, f32[16,32]{1,0:T(8,128)} %weight_hbm.1, f32[16,32]{1,0:T(8,128)} %residual_hbm.1, f32[8,128]{1,0:T(8,128)} %bitcast.9, s32[1,32]{1,0:T(1,128)} %bitcast.10, s32[1,16]{1,0:T(1,128)} %bitcast.11), custom_call_target="tpu_custom_call" | custom-call | tf_op jit(solution)/shard_map/pallas_call | solution.py:353
  16.2 0.5 %slice_bitcast_fusion = (f32[16]{0:T(128)}, f32[16]{0:T(128)}) fusion(f32[2,16]{1,0:T(2,128)S(1)} %shard_map.86), kind=kLoop, calls=%fused_computation | loop fusion | bytes 256 | tf_op jit(solution)/shard_map/squeeze | solution.py:391

commit v3 on v2

v3 whole, which is shorter than its diff:
```python
import functools

import jax
import jax.numpy as jnp
from jax import lax
from jax.experimental import pallas as pl
from jax.experimental.pallas import tpu as pltpu
from jax.sharding import PartitionSpec as P

BLK = 128
MESH = pl.DeviceIdType.MESH
STATS = 5
SCORE = 16
PAIR = 2
CHUNK = 2
ORDER = ((1, 0), (1, 3), (0, 0), (0, 3), (1, 2), (1, 1), (0, 2), (0, 1))


def lane_sum(row):
    return jnp.sum(row, axis=1, keepdims=True)


def owner_range(samp_size, local_blocks):
    low = samp_size // 4
    size = max(1, samp_size // 2)
    while local_blocks % size:
        size -= 1
    return low, size


def flip(samp, step):
    peer, bit = samp, 1
    while bit <= step:
        if step & bit:
            peer = peer + bit * (1 - 2 * lax.rem(lax.div(samp, bit), 2))
        bit *= 2
    return peer


def kernel(
    samp_size,
    gene_size,
    owner_low,
    owner_size,
    genotypes_hbm,
    freq_hbm,
    weight_hbm,
    residual_hbm,
    variant_hbm,
    block_gene_hbm,
    counts_hbm,
    both_ref,
    words_in,
    weight_in,
    residual_in,
    block_gene_in,
    counts_in,
    params,
    tile_out,
    tiles,
    words,
    centers,
    pair_weight,
    row_out,
    rows,
    load_sem,
    send_sem,
    tile_sem,
    word_sem,
    param_sem,
    row_sem,
):
    samp = lax.axis_index("samp")
    gene = lax.axis_index("gene")
    side = lax.rem(gene, PAIR)
    lead = gene - side + (PAIR - 1)
    fields, local_rows = weight_in.shape
    group = BLK // local_rows
    depth = fields // group
    local_blocks = params.shape[2]
    owned = local_blocks // owner_size
    owner_high = owner_low + owner_size
    genes = counts_in.shape[1]
    width = row_out.shape[1]
    leads = side == PAIR - 1
    in_range = jnp.logical_and(samp >= owner_low, samp < owner_high)
    owns = jnp.logical_and(leads, in_range)
    helps = jnp.logical_and(jnp.logical_not(leads), in_range)
    place = samp - owner_low
    pairs = gene_size // PAIR
    row_count = owner_size * pairs

    loads = [
        pltpu.make_async_copy(source, target, load_sem.at[number])
        for number, source, target in (
            (0, genotypes_hbm, words_in),
            (1, weight_hbm, weight_in),
            (1, residual_hbm, residual_in),
            (2, freq_hbm, params.at[side, 0]),
            (2, variant_hbm, params.at[side, 1]),
            (2, block_gene_hbm, block_gene_in),
            (2, counts_hbm, counts_in),
        )
    ]
    for load in loads[1:] + loads[:1]:
        load.start()

    def signal(semaphore, samp_to, gene_to):
        pl.semaphore_signal(
            semaphore,
            inc=1,
            device_id={"samp": samp_to, "gene": gene_to},
            device_id_type=MESH,
        )

    barrier = pltpu.get_barrier_semaphore()

    @pl.when(owns)
    def _():
        for other in range(1, PAIR):
            signal(barrier, samp, gene - other)

        @pl.loop(1, samp_size)
        def _(step):
            for other in range(PAIR):
                signal(barrier, lax.rem(samp + step, samp_size), gene - other)

    for step in range(1, pairs):
        signal(barrier, samp, lax.rem(gene + step * PAIR, gene_size))

    loads[1].wait()
    loads[2].wait()
    own_tile = jnp.concatenate(
        [
            jnp.concatenate(
                [part[lanes * depth : (lanes + 1) * depth] for lanes in range(group)], axis=1
            )
            for part in (weight_in[...], residual_in[...])
        ],
        axis=0,
    )
    tile_out[...] = own_tile
    tiles[samp] = own_tile

    pl.semaphore_wait(barrier, jnp.where(owns, owner_size - 1, owner_size) + pairs - 1)

    chunk = lax.div(samp, CHUNK)

    def tile_copy(owner):
        return pltpu.make_async_remote_copy(
            src_ref=tile_out,
            dst_ref=tiles.at[samp],
            send_sem=send_sem,
            recv_sem=tile_sem.at[chunk],
            device_id={"samp": owner, "gene": lead},
            device_id_type=MESH,
        )

    def word_copy(owner):
        start = pl.multiple_of((owner - owner_low) * (owned * BLK), BLK)
        return pltpu.make_async_remote_copy(
            src_ref=words_in.at[:, pl.ds(start, owned * BLK)],
            dst_ref=words.at[side, samp],
            send_sem=send_sem,
            recv_sem=word_sem.at[side, chunk],
            device_id={"samp": owner, "gene": lead},
            device_id_type=MESH,
        )

    upward = 2 * samp < 2 * owner_low + owner_size

    def to_owners(send, condition):
        for order in range(owner_size):
            owner = jnp.where(upward, owner_high - 1 - order, owner_low + order)

            @pl.when(condition(owner))
            def _(owner=owner):
                send(owner).start()

    to_owners(tile_copy, lambda owner: jnp.logical_and(leads, owner != samp))
    loads[0].wait()
    to_owners(
        word_copy, lambda owner: jnp.logical_or(jnp.logical_not(leads), owner != samp)
    )
    for load in loads[3:]:
        load.wait()

    @pl.when(helps)
    def _():
        pltpu.make_async_remote_copy(
            src_ref=params.at[side],
            dst_ref=params.at[side],
            send_sem=send_sem,
            recv_sem=param_sem,
            device_id={"samp": samp, "gene": lead},
            device_id_type=MESH,
        ).start()

    @pl.when(owns)
    def _():
        own_start = pl.multiple_of(place * (owned * BLK), BLK)
        words[PAIR - 1, samp] = words_in[:, pl.ds(own_start, owned * BLK)]
        if PAIR > 1:
            landed = params.at[pl.ds(0, PAIR - 1)]
            pltpu.make_async_copy(landed, landed, param_sem).wait()
        block_gene = block_gene_in[...].astype(jnp.float32)
        counts = counts_in[...].astype(jnp.float32)
        block_lane = lax.broadcasted_iota(jnp.int32, block_gene.shape, 1)
        gene_lane = lax.broadcasted_iota(jnp.int32, counts.shape, 1).astype(jnp.float32)
        column = lax.broadcasted_iota(jnp.int32, (1, BLK), 1).astype(jnp.float32)
        stat_sub = lax.broadcasted_iota(jnp.int32, (8, width), 0)
        stat_lane = lax.broadcasted_iota(jnp.int32, (8, width), 1) - stat_sub * genes
        effective, places = [], []
        for number in range(PAIR * owned):
            from_side, block = divmod(number, owned)
            local_block = place * owned + block
            block_id = (lead - (PAIR - 1) + from_side) * local_blocks + local_block
            gene_of = lane_sum(jnp.where(block_lane == block_id, block_gene, 0.0))
            first = lane_sum(jnp.where(block_gene < gene_of, 1.0, 0.0))
            counted = lane_sum(jnp.where(gene_lane == gene_of, counts, 0.0))
            block_float = jnp.zeros((1, 1), jnp.float32) + block_id.astype(jnp.float32)
            live = (block_float - first) * BLK + column < counted
            weights = jnp.where(live, params[from_side, 1, pl.ds(local_block, 1), :], 0.0)
            effective.append(weights)
            across = jnp.broadcast_to(weights, (BLK, BLK))
            pair_weight[number] = across * across.T
            freq = params[from_side, 0, pl.ds(local_block, 1), :]
            center = 2.0 * jnp.broadcast_to(freq, (BLK, BLK)).T
            for level in range(depth):
                centers[number, level] = center * float(4**level)
            member = stat_lane.astype(jnp.float32) == gene_of
            places.append(jnp.where(member & (stat_sub < STATS), 1.0, 0.0))

        def land(buffer, semaphore):
            pltpu.make_async_copy(buffer, buffer, semaphore).wait()

        def unpack(from_side, peer, power):
            tile = tiles[peer]
            weight, resid = tile[:depth], tile[depth:]
            root = jnp.sqrt(weight)
            score = root * resid
            values = []
            for block in range(owned):
                part = words[from_side, peer, :, block * BLK : (block + 1) * BLK]
                turned = jnp.concatenate(
                    [lax.shift_right_logical(part, 2 * depth * lanes) for lanes in range(group)],
                    axis=0,
                ).T
                levels = []
                for level in range(depth):
                    dosage = jnp.bitwise_and(turned, 3 << (2 * level)).astype(jnp.float32)
                    scale = root[level : level + 1] * float(4**-level)
                    center = centers[from_side * owned + block, level]
                    levels.append(((dosage - center) * scale).astype(jnp.bfloat16))
                values.append(jnp.concatenate(levels, axis=1))
            scores = jnp.concatenate(
                [
                    jnp.broadcast_to(score[level : level + 1], (SCORE, BLK)).astype(jnp.bfloat16)
                    for level in range(depth)
                ],
                axis=1,
            )
            if from_side == PAIR - 1:
                power = power + weight * resid * resid
            return (from_side, values, scores), power

        def multiply(unpacked, totals):
            from_side, values, scores = unpacked
            totals = list(totals)
            for block in range(owned):
                number = from_side * owned + block
                totals[number] = totals[number] + lax.dot_general(
                    jnp.concatenate([values[block], scores], axis=0),
                    values[block],
                    (((1,), (1,)), ((), ())),
                    preferred_element_type=jnp.float32,
                )
            return tuple(totals)

        def wait_chunk(from_side, from_chunk, own):
            first = from_chunk * CHUNK
            if from_side < PAIR - 1:
                land(words.at[from_side, pl.ds(first, CHUNK)], word_sem.at[from_side, from_chunk])
            elif own:
                peer = flip(samp, 1)
                land(tiles.at[peer], tile_sem.at[from_chunk])
                land(words.at[from_side, peer], word_sem.at[from_side, from_chunk])
            else:
                land(tiles.at[pl.ds(first, CHUNK)], tile_sem.at[from_chunk])
                land(words.at[from_side, pl.ds(first, CHUNK)], word_sem.at[from_side, from_chunk])

        chunks = samp_size // CHUNK
        totals = tuple(jnp.zeros((BLK + SCORE, BLK), jnp.float32) for _ in range(PAIR * owned))
        power = jnp.zeros((depth, BLK), jnp.float32)
        if chunks == 4:
            waiting = None
            for from_side, step in ORDER:
                from_chunk = flip(chunk, step)
                wait_chunk(from_side, from_chunk, step == 0)
                for member in range(CHUNK):
                    ahead, power = unpack(from_side, from_chunk * CHUNK + member, power)
                    if waiting is not None:
                        totals = multiply(waiting, totals)
                    waiting = ahead
            totals = multiply(waiting, totals)
        else:

            def add_chunk(from_chunk, totals, power, own):
                for from_side in reversed(range(PAIR)):
                    wait_chunk(from_side, from_chunk, own)
                    for member in range(CHUNK):
                        ahead, power = unpack(from_side, from_chunk * CHUNK + member, power)
                        totals = multiply(ahead, totals)
                return totals, power

            totals, power = lax.fori_loop(
                1,
                chunks,
                lambda step, carry: add_chunk(lax.rem(chunk + step, chunks), *carry, False),
                add_chunk(chunk, totals, power, True),
            )

        message = jnp.zeros((8, width), jnp.float32)
        diagonal = lax.broadcasted_iota(jnp.int32, (BLK, BLK), 0) == lax.broadcasted_iota(
            jnp.int32, (BLK, BLK), 1
        )
        for number in range(PAIR * owned):
            total = totals[number]
            weighted = total[:BLK] * pair_weight[number]
            score = effective[number] * total[BLK : BLK + 1]
            sums = [
                score,
                jnp.sum(weighted, axis=0, keepdims=True),
                score * score,
                jnp.sum(jnp.where(diagonal, weighted, 0.0), axis=0, keepdims=True),
                jnp.sum(weighted * weighted, axis=0, keepdims=True),
                jnp.zeros((8 - STATS, BLK), jnp.float32),
            ]
            message = message + lane_sum(jnp.concatenate(sums, axis=0)) * places[number]
        squares = lane_sum(jnp.sum(power, axis=0, keepdims=True))
        lane = lax.broadcasted_iota(jnp.int32, (1, width), 1)
        reports = jnp.logical_and(place == 0, lead == PAIR - 1).astype(jnp.float32)
        row = jnp.sum(message, axis=0, keepdims=True) + jnp.where(
            lane == STATS * genes, squares * reports, 0.0
        )
        row_out[...] = row
        slot = place * pairs + lax.div(gene, PAIR)
        rows[slot] = row

        @pl.loop(0, samp_size)
        def _(samp_to):
            for gene_to in range(gene_size):

                @pl.when(jnp.logical_or(samp_to != samp, gene_to != gene))
                def _(gene_to=gene_to):
                    pltpu.make_async_remote_copy(
                        src_ref=row_out,
                        dst_ref=rows.at[slot],
                        send_sem=send_sem,
                        recv_sem=row_sem,
                        device_id={"samp": samp_to, "gene": gene_to},
                        device_id_type=MESH,
                    ).start()

    @pl.when(owns)
    def _():
        landed = rows.at[pl.ds(0, row_count - 1)]
        pltpu.make_async_copy(landed, landed, row_sem).wait()

    @pl.when(jnp.logical_not(owns))
    def _():
        pltpu.make_async_copy(rows, rows, row_sem).wait()

    totals = jnp.sum(rows[...], axis=0)
    parts = [totals[:, stat * genes : (stat + 1) * genes] for stat in range(STATS)]
    variance = totals[:, STATS * genes : STATS * genes + 1] / (fields * local_rows * samp_size)
    both_ref[0:1] = parts[0] / jnp.sqrt(variance * parts[1])
    both_ref[1:2] = (parts[2] - variance * parts[3]) / (
        variance * jnp.sqrt(2.0 * parts[4])
    )

    def sent(buffer, count):
        @pl.loop(0, count)
        def _(_):
            pltpu.make_async_copy(buffer, buffer, send_sem).wait()

    targets = jnp.where(owns, owner_size - 1, owner_size)
    sent(words.at[0, 0], targets)
    sent(tile_out, jnp.where(leads, targets, 0))
    sent(params.at[0], jnp.where(helps, 1, 0))
    sent(row_out, jnp.where(owns, samp_size * gene_size - 1, 0))


def solution(mesh):
    samp_size, gene_size = mesh.shape["samp"], mesh.shape["gene"]

    def local(
        genotypes, allele_freq, sample_weight, residual, variant_weight, block_gene, gene_variants
    ):
        local_rows, columns = genotypes.shape
        local_blocks = columns // BLK
        fields = sample_weight.shape[0]
        genes = gene_variants.shape[0]
        depth = fields * local_rows // BLK
        width = -(-(STATS * genes + 1) // BLK) * BLK
        owner_low, owner_size = owner_range(samp_size, local_blocks)
        owned = local_blocks // owner_size
        both = pl.pallas_call(
            functools.partial(kernel, samp_size, gene_size, owner_low, owner_size),
            out_shape=pltpu.VMEM((2, genes), jnp.float32),
            in_specs=[pl.BlockSpec(memory_space=pl.ANY)] * 7,
            out_specs=pl.BlockSpec(memory_space=pltpu.VMEM),
            scratch_shapes=[
                pltpu.VMEM((local_rows, columns), jnp.int32),
                pltpu.VMEM((fields, local_rows), jnp.float32),
                pltpu.VMEM((fields, local_rows), jnp.float32),
                pltpu.VMEM((1, block_gene.shape[0]), jnp.int32),
                pltpu.VMEM((1, genes), jnp.int32),
                pltpu.VMEM((PAIR, 2, local_blocks, BLK), jnp.float32),
                pltpu.VMEM((2 * depth, BLK), jnp.float32),
                pltpu.VMEM((samp_size, 2 * depth, BLK), jnp.float32),
                pltpu.VMEM((PAIR, samp_size, local_rows, owned * BLK), jnp.int32),
                pltpu.VMEM((PAIR * owned, depth, BLK, BLK), jnp.float32),
                pltpu.VMEM((PAIR * owned, BLK, BLK), jnp.float32),
                pltpu.VMEM((1, width), jnp.float32),
                pltpu.VMEM((owner_size * gene_size // PAIR, 1, width), jnp.float32),
                pltpu.SemaphoreType.DMA((3,)),
                pltpu.SemaphoreType.DMA,
                pltpu.SemaphoreType.DMA((samp_size // CHUNK,)),
                pltpu.SemaphoreType.DMA((PAIR, samp_size // CHUNK)),
                pltpu.SemaphoreType.DMA,
                pltpu.SemaphoreType.DMA,
            ],
            compiler_params=pltpu.CompilerParams(collective_id=0, has_side_effects=True),
        )(
            genotypes,
            allele_freq.reshape(local_blocks, BLK),
            sample_weight,
            residual,
            variant_weight.reshape(local_blocks, BLK),
            block_gene.reshape(1, -1),
            gene_variants.reshape(1, -1),
        )
        return both[0], both[1]

    placed = (P("samp", "gene"), P("gene"), P(None, "samp"), P(None, "samp"), P("gene"), P(), P())
    return jax.shard_map(local, mesh=mesh, in_specs=placed, out_specs=(P(), P()), check_vma=False)
```

time: 16.8 us -> 16.1 us (0.958)
  Pallas kernels: 15.5 us -> 14.8 us
    pallas_call x1, Pallas kernels: 15.5 us -> 14.8 us  [local(): pl.pallas_call(functools.partial(kernel, samp_size, gene_size, owner_low,...]
where the time goes in v3:
time: 16.1 us; the launch traced here: 15.9 us
  Pallas kernels  14.8 us (92%)
  between operations  0.64 us (4%)
  local copies, waits for them, and re-layouts  0.52 us (3%)
    pallas_call x1, Pallas kernels, local(): pl.pallas_call(functools.partial(kernel, samp_size, gene_size, owner_low,...  14.8 us
    squeeze x1, local copies, waits for them, and re-layouts, local(): return (both[0], both[1])  0.52 us

profile of v3, /device:TPU:0, one launch (start us, length us, event | category | flops | bytes accessed | tf_op | source)
XLA Modules:
  0.0 15.9 jit_solution(9791149793282609092)
XLA Ops:
  0.6 14.8 %shard_map.86 = f32[2,16]{1,0:T(2,128)S(1)} custom-call(s32[32,1024]{1,0:T(8,128)} %genotypes_hbm.1, f32[8,128]{1,0:T(8,128)} %bitcast.8, f32[16,32]{1,0:T(8,128)} %weight_hbm.1, f32[16,32]{1,0:T(8,128)} %residual_hbm.1, f32[8,128]{1,0:T(8,128)} %bitcast.9, s32[1,32]{1,0:T(1,128)} %bitcast.10, s32[1,16]{1,0:T(1,128)} %bitcast.11), custom_call_target="tpu_custom_call" | custom-call | tf_op jit(solution)/shard_map/pallas_call | solution.py:408
  15.4 0.5 %slice_bitcast_fusion = (f32[16]{0:T(128)}, f32[16]{0:T(128)}) fusion(f32[2,16]{1,0:T(2,128)S(1)} %shard_map.86), kind=kLoop, calls=%fused_computation | loop fusion | bytes 256 | tf_op jit(solution)/shard_map/squeeze | solution.py:444

commit v4 on v3

v4 whole, which is shorter than its diff:
```python
import functools

import jax
import jax.numpy as jnp
from jax import lax
from jax.experimental import pallas as pl
from jax.experimental.pallas import tpu as pltpu
from jax.sharding import PartitionSpec as P

BLK = 128
MESH = pl.DeviceIdType.MESH
STATS = 5
SCORE = 16
PAIR = 2
CHUNK = 2
LEAD_ORDER = ((1, 0), (1, 3), (1, 2), (1, 1), (0, 0), (0, 3), (0, 2), (0, 1))
HELP_ORDER = ((0, 0), (0, 3), (0, 2), (0, 1))


def lane_sum(row):
    return jnp.sum(row, axis=1, keepdims=True)


def owner_range(samp_size, local_blocks):
    low = samp_size // 4
    size = max(1, samp_size // 2)
    while local_blocks % (PAIR * size) and size > 1:
        size -= 1
    return low, size


def flip(samp, step):
    peer, bit = samp, 1
    while bit <= step:
        if step & bit:
            peer = peer + bit * (1 - 2 * lax.rem(lax.div(samp, bit), 2))
        bit *= 2
    return peer


def kernel(
    samp_size,
    gene_size,
    owner_low,
    owner_size,
    genotypes_hbm,
    freq_hbm,
    weight_hbm,
    residual_hbm,
    variant_hbm,
    block_gene_hbm,
    counts_hbm,
    both_ref,
    words_in,
    weight_in,
    residual_in,
    block_gene_in,
    counts_in,
    params,
    tile_out,
    tiles,
    lead_words,
    kept_words,
    given_words,
    centers,
    pair_weight,
    row_out,
    rows,
    load_sem,
    send_sem,
    tile_sem,
    word_sem,
    param_sem,
    row_sem,
    answer_sem,
    known_sem,
):
    samp = lax.axis_index("samp")
    gene = lax.axis_index("gene")
    side = lax.rem(gene, PAIR)
    lead = gene - side + (PAIR - 1)
    fields, local_rows = weight_in.shape
    group = BLK // local_rows
    depth = fields // group
    local_blocks = params.shape[2]
    owned = local_blocks // owner_size
    taken = owned // 2
    owner_high = owner_low + owner_size
    genes = counts_in.shape[1]
    width = row_out.shape[1]
    leads = side == PAIR - 1
    in_range = jnp.logical_and(samp >= owner_low, samp < owner_high)
    owns = jnp.logical_and(leads, in_range)
    helps = jnp.logical_and(jnp.logical_not(leads), in_range)
    place = samp - owner_low
    row_count = rows.shape[0]

    loads = [
        pltpu.make_async_copy(source, target, load_sem.at[number])
        for number, source, target in (
            (0, genotypes_hbm, words_in),
            (1, weight_hbm, weight_in),
            (1, residual_hbm, residual_in),
            (2, freq_hbm, params.at[side, 0]),
            (2, variant_hbm, params.at[side, 1]),
            (2, block_gene_hbm, block_gene_in),
            (2, counts_hbm, counts_in),
        )
    ]
    for load in loads[1:] + loads[:1]:
        load.start()

    def signal(semaphore, samp_to, gene_to):
        pl.semaphore_signal(
            semaphore,
            inc=1,
            device_id={"samp": samp_to, "gene": gene_to},
            device_id_type=MESH,
        )

    barrier = pltpu.get_barrier_semaphore()

    @pl.when(leads)
    def _():
        signal(barrier, samp, gene - 1)

    @pl.when(in_range)
    def _():
        @pl.loop(1, samp_size)
        def _(step):
            samp_to = lax.rem(samp + step, samp_size)
            signal(barrier, samp_to, gene)

            @pl.when(leads)
            def _():
                signal(barrier, samp_to, gene - 1)

    for gene_to in range(PAIR, gene_size):

        @pl.when(gene_to > lead)
        def _(gene_to=gene_to):
            signal(barrier, samp, gene_to)

    loads[1].wait()
    loads[2].wait()
    own_tile = jnp.concatenate(
        [
            jnp.concatenate(
                [part[lanes * depth : (lanes + 1) * depth] for lanes in range(group)], axis=1
            )
            for part in (weight_in[...], residual_in[...])
        ],
        axis=0,
    )
    tile_out[...] = own_tile
    tiles[samp] = own_tile

    targets = jnp.where(in_range, owner_size - 1, owner_size)
    earlier = lead - (PAIR - 1)
    pl.semaphore_wait(barrier, jnp.where(leads, targets, 2 * targets + 1) + earlier)

    chunk = lax.div(samp, CHUNK)

    def tile_copy(owner):
        return pltpu.make_async_remote_copy(
            src_ref=tile_out,
            dst_ref=tiles.at[samp],
            send_sem=send_sem,
            recv_sem=tile_sem.at[chunk],
            device_id={"samp": owner, "gene": gene},
            device_id_type=MESH,
        )

    def word_copy(target, first, count, gene_to):
        def copy(owner):
            start = pl.multiple_of(((owner - owner_low) * owned + first) * BLK, BLK)
            return pltpu.make_async_remote_copy(
                src_ref=words_in.at[:, pl.ds(start, count * BLK)],
                dst_ref=target.at[samp],
                send_sem=send_sem,
                recv_sem=word_sem.at[side, chunk],
                device_id={"samp": owner, "gene": gene_to},
                device_id_type=MESH,
            )

        return copy

    upward = 2 * samp < 2 * owner_low + owner_size

    def to_owner(send, order, here=False):
        owner = jnp.where(upward, owner_high - 1 - order, owner_low + order)
        if here:
            send(owner).start()
        else:

            @pl.when(owner != samp)
            def _():
                send(owner).start()

    def to_owners(send):
        for order in range(owner_size):
            to_owner(send, order)

    to_owners(tile_copy)
    loads[0].wait()

    @pl.when(leads)
    def _():
        to_owners(word_copy(lead_words, 0, owned, gene))

    @pl.when(jnp.logical_not(leads))
    def _():
        for order in range(owner_size):
            to_owner(word_copy(kept_words, taken, owned - taken, gene), order)
            if taken:
                to_owner(word_copy(given_words, 0, taken, lead), order, True)

    for gene_to in range(gene_size - PAIR):

        @pl.when(gene_to < earlier)
        def _(gene_to=gene_to):
            signal(answer_sem, samp, gene_to)

    for load in loads[3:]:
        load.wait()
    later = gene_size - 1 - lead

    @pl.when(jnp.logical_and(helps, taken > 0))
    def _():
        pltpu.make_async_remote_copy(
            src_ref=params.at[0],
            dst_ref=params.at[0],
            send_sem=send_sem,
            recv_sem=param_sem,
            device_id={"samp": samp, "gene": lead},
            device_id_type=MESH,
        ).start()

    @pl.when(later > 0)
    def _():
        pl.semaphore_wait(answer_sem, later)

        @pl.loop(owner_low, owner_high)
        def _(owner):
            @pl.when(owner != samp)
            def _():
                signal(known_sem, owner, gene)

    def own(streams, order):
        block_gene = block_gene_in[...].astype(jnp.float32)
        counts = counts_in[...].astype(jnp.float32)
        block_lane = lax.broadcasted_iota(jnp.int32, block_gene.shape, 1)
        gene_lane = lax.broadcasted_iota(jnp.int32, counts.shape, 1).astype(jnp.float32)
        column = lax.broadcasted_iota(jnp.int32, (1, BLK), 1).astype(jnp.float32)
        stat_sub = lax.broadcasted_iota(jnp.int32, (8, width), 0)
        stat_lane = lax.broadcasted_iota(jnp.int32, (8, width), 1) - stat_sub * genes
        effective, places, numbers = [], [], {}
        for from_side, (buffer, first_block, count) in streams.items():
            for block in range(count):
                number = numbers[from_side, block] = len(numbers)
                local_block = place * owned + first_block + block
                block_id = (lead - (PAIR - 1) + from_side) * local_blocks + local_block
                gene_of = lane_sum(jnp.where(block_lane == block_id, block_gene, 0.0))
                first = lane_sum(jnp.where(block_gene < gene_of, 1.0, 0.0))
                counted = lane_sum(jnp.where(gene_lane == gene_of, counts, 0.0))
                block_float = jnp.zeros((1, 1), jnp.float32) + block_id.astype(jnp.float32)
                live = (block_float - first) * BLK + column < counted
                weights = jnp.where(live, params[from_side, 1, pl.ds(local_block, 1), :], 0.0)
                effective.append(weights)
                across = jnp.broadcast_to(weights, (BLK, BLK))
                pair_weight[number] = across * across.T
                freq = params[from_side, 0, pl.ds(local_block, 1), :]
                center = 2.0 * jnp.broadcast_to(freq, (BLK, BLK)).T
                for level in range(depth):
                    centers[number, level] = center * float(4**level)
                member = stat_lane.astype(jnp.float32) == gene_of
                places.append(jnp.where(member & (stat_sub < STATS), 1.0, 0.0))

        def land(buffer, semaphore):
            pltpu.make_async_copy(buffer, buffer, semaphore).wait()

        def unpack(from_side, peer, power):
            tile = tiles[peer]
            weight, resid = tile[:depth], tile[depth:]
            root = jnp.sqrt(weight)
            score = root * resid
            values = []
            buffer, _, count = streams[from_side]
            for block in range(count):
                part = buffer[peer, :, block * BLK : (block + 1) * BLK]
                turned = jnp.concatenate(
                    [lax.shift_right_logical(part, 2 * depth * lanes) for lanes in range(group)],
                    axis=0,
                ).T
                levels = []
                for level in range(depth):
                    dosage = jnp.bitwise_and(turned, 3 << (2 * level)).astype(jnp.float32)
                    scale = root[level : level + 1] * float(4**-level)
                    center = centers[numbers[from_side, block], level]
                    levels.append(((dosage - center) * scale).astype(jnp.bfloat16))
                values.append(jnp.concatenate(levels, axis=1))
            scores = jnp.concatenate(
                [
                    jnp.broadcast_to(score[level : level + 1], (SCORE, BLK)).astype(jnp.bfloat16)
                    for level in range(depth)
                ],
                axis=1,
            )
            if from_side == main_side:
                power = power + weight * resid * resid
            return (from_side, values, scores), power

        def multiply(unpacked, totals):
            from_side, values, scores = unpacked
            totals = list(totals)
            for block in range(streams[from_side][2]):
                number = numbers[from_side, block]
                totals[number] = totals[number] + lax.dot_general(
                    jnp.concatenate([values[block], scores], axis=0),
                    values[block],
                    (((1,), (1,)), ((), ())),
                    preferred_element_type=jnp.float32,
                )
            return tuple(totals)

        def wait_chunk(from_side, from_chunk, own):
            first = from_chunk * CHUNK
            buffer = streams[from_side][0]
            if from_side != main_side:
                land(buffer.at[pl.ds(first, CHUNK)], word_sem.at[from_side, from_chunk])
            elif own:
                peer = flip(samp, 1)
                land(tiles.at[peer], tile_sem.at[from_chunk])
                land(buffer.at[peer], word_sem.at[from_side, from_chunk])
            else:
                land(tiles.at[pl.ds(first, CHUNK)], tile_sem.at[from_chunk])
                land(buffer.at[pl.ds(first, CHUNK)], word_sem.at[from_side, from_chunk])

        main_side = max(streams)
        buffer, first_block, count = streams[main_side]
        own_start = pl.multiple_of((place * owned + first_block) * BLK, BLK)
        buffer[samp] = words_in[:, pl.ds(own_start, count * BLK)]
        diagonal = lax.broadcasted_iota(jnp.int32, (BLK, BLK), 0) == lax.broadcasted_iota(
            jnp.int32, (BLK, BLK), 1
        )

        def finish(from_side, totals, message):
            for block in range(streams[from_side][2]):
                number = numbers[from_side, block]
                total = totals[number]
                weighted = total[:BLK] * pair_weight[number]
                score = effective[number] * total[BLK : BLK + 1]
                sums = [
                    score,
                    jnp.sum(weighted, axis=0, keepdims=True),
                    score * score,
                    jnp.sum(jnp.where(diagonal, weighted, 0.0), axis=0, keepdims=True),
                    jnp.sum(weighted * weighted, axis=0, keepdims=True),
                    jnp.zeros((8 - STATS, BLK), jnp.float32),
                ]
                message = message + lane_sum(jnp.concatenate(sums, axis=0)) * places[number]
            return message

        chunks = samp_size // CHUNK
        totals = tuple(jnp.zeros((BLK + SCORE, BLK), jnp.float32) for _ in numbers)
        power = jnp.zeros((depth, BLK), jnp.float32)
        message = jnp.zeros((8, width), jnp.float32)
        finished = set()
        if chunks == 4:
            waiting = None
            for place_in_order, (from_side, step) in enumerate(order):
                from_chunk = flip(chunk, step)
                wait_chunk(from_side, from_chunk, step == 0)
                for member in range(CHUNK):
                    ahead, power = unpack(from_side, from_chunk * CHUNK + member, power)
                    if waiting is not None:
                        totals = multiply(waiting, totals)
                    waiting = ahead
                for done in streams:
                    left = [turn for turn in order[place_in_order:] if turn[0] == done]
                    if not left and done not in finished and done != from_side:
                        message = finish(done, totals, message)
                        finished.add(done)
            totals = multiply(waiting, totals)
        else:

            def add_chunk(from_chunk, totals, power, own):
                for from_side in sorted(streams, reverse=True):
                    wait_chunk(from_side, from_chunk, own)
                    for member in range(CHUNK):
                        ahead, power = unpack(from_side, from_chunk * CHUNK + member, power)
                        totals = multiply(ahead, totals)
                return totals, power

            totals, power = lax.fori_loop(
                1,
                chunks,
                lambda step, carry: add_chunk(lax.rem(chunk + step, chunks), *carry, False),
                add_chunk(chunk, totals, power, True),
            )

        for from_side in streams:
            if from_side not in finished:
                message = finish(from_side, totals, message)
        squares = lane_sum(jnp.sum(power, axis=0, keepdims=True))
        lane = lax.broadcasted_iota(jnp.int32, (1, width), 1)
        reports = jnp.logical_and(place == 0, gene == PAIR - 1).astype(jnp.float32)
        row = jnp.sum(message, axis=0, keepdims=True) + jnp.where(
            lane == STATS * genes, squares * reports, 0.0
        )
        @pl.when(later > 0)
        def _():
            pl.semaphore_wait(known_sem, samp_size - 1)

        row_out[...] = row
        slot = place * gene_size + gene
        rows[slot] = row

        @pl.loop(0, samp_size)
        def _(samp_to):
            for gene_to in range(gene_size):

                @pl.when(jnp.logical_or(samp_to != samp, gene_to != gene))
                def _(gene_to=gene_to):
                    pltpu.make_async_remote_copy(
                        src_ref=row_out,
                        dst_ref=rows.at[slot],
                        send_sem=send_sem,
                        recv_sem=row_sem,
                        device_id={"samp": samp_to, "gene": gene_to},
                        device_id_type=MESH,
                    ).start()

    lead_streams = {PAIR - 1: (lead_words, 0, owned)}
    if taken:
        lead_streams[0] = (given_words, 0, taken)

    @pl.when(owns)
    def _():
        if taken:
            landed = params.at[0]
            pltpu.make_async_copy(landed, landed, param_sem).wait()
        own(lead_streams, [turn for turn in LEAD_ORDER if turn[0] in lead_streams])

    @pl.when(helps)
    def _():
        own({0: (kept_words, taken, owned - taken)}, HELP_ORDER)

    @pl.when(in_range)
    def _():
        landed = rows.at[pl.ds(0, row_count - 1)]
        pltpu.make_async_copy(landed, landed, row_sem).wait()

    @pl.when(jnp.logical_not(in_range))
    def _():
        pltpu.make_async_copy(rows, rows, row_sem).wait()

    totals = jnp.sum(rows[...], axis=0)
    parts = [totals[:, stat * genes : (stat + 1) * genes] for stat in range(STATS)]
    variance = totals[:, STATS * genes : STATS * genes + 1] / (fields * local_rows * samp_size)
    both_ref[0:1] = parts[0] / jnp.sqrt(variance * parts[1])
    both_ref[1:2] = (parts[2] - variance * parts[3]) / (
        variance * jnp.sqrt(2.0 * parts[4])
    )

    def sent(buffer, count):
        @pl.loop(0, count)
        def _(_):
            pltpu.make_async_copy(buffer, buffer, send_sem).wait()

    sent(tile_out, targets)
    sent(lead_words.at[0], jnp.where(leads, targets, 0))
    sent(kept_words.at[0], jnp.where(leads, 0, targets))
    if taken:
        sent(given_words.at[0], jnp.where(leads, 0, owner_size))
        sent(params.at[0], jnp.where(helps, 1, 0))
    sent(row_out, jnp.where(in_range, samp_size * gene_size - 1, 0))


def solution(mesh):
    samp_size, gene_size = mesh.shape["samp"], mesh.shape["gene"]

    def local(
        genotypes, allele_freq, sample_weight, residual, variant_weight, block_gene, gene_variants
    ):
        local_rows, columns = genotypes.shape
        local_blocks = columns // BLK
        fields = sample_weight.shape[0]
        genes = gene_variants.shape[0]
        depth = fields * local_rows // BLK
        width = -(-(STATS * genes + 1) // BLK) * BLK
        owner_low, owner_size = owner_range(samp_size, local_blocks)
        owned = local_blocks // owner_size
        taken = owned // 2
        both = pl.pallas_call(
            functools.partial(kernel, samp_size, gene_size, owner_low, owner_size),
            out_shape=pltpu.VMEM((2, genes), jnp.float32),
            in_specs=[pl.BlockSpec(memory_space=pl.ANY)] * 7,
            out_specs=pl.BlockSpec(memory_space=pltpu.VMEM),
            scratch_shapes=[
                pltpu.VMEM((local_rows, columns), jnp.int32),
                pltpu.VMEM((fields, local_rows), jnp.float32),
                pltpu.VMEM((fields, local_rows), jnp.float32),
                pltpu.VMEM((1, block_gene.shape[0]), jnp.int32),
                pltpu.VMEM((1, genes), jnp.int32),
                pltpu.VMEM((PAIR, 2, local_blocks, BLK), jnp.float32),
                pltpu.VMEM((2 * depth, BLK), jnp.float32),
                pltpu.VMEM((samp_size, 2 * depth, BLK), jnp.float32),
                pltpu.VMEM((samp_size, local_rows, owned * BLK), jnp.int32),
                pltpu.VMEM((samp_size, local_rows, (owned - taken) * BLK), jnp.int32),
                pltpu.VMEM((samp_size, local_rows, max(taken, 1) * BLK), jnp.int32),
                pltpu.VMEM((owned + taken, depth, BLK, BLK), jnp.float32),
                pltpu.VMEM((owned + taken, BLK, BLK), jnp.float32),
                pltpu.VMEM((1, width), jnp.float32),
                pltpu.VMEM((owner_size * gene_size, 1, width), jnp.float32),
                pltpu.SemaphoreType.DMA((3,)),
                pltpu.SemaphoreType.DMA,
                pltpu.SemaphoreType.DMA((samp_size // CHUNK,)),
                pltpu.SemaphoreType.DMA((PAIR, samp_size // CHUNK)),
                pltpu.SemaphoreType.DMA,
                pltpu.SemaphoreType.DMA,
                pltpu.SemaphoreType.REGULAR,
                pltpu.SemaphoreType.REGULAR,
            ],
            compiler_params=pltpu.CompilerParams(collective_id=0, has_side_effects=True),
        )(
            genotypes,
            allele_freq.reshape(local_blocks, BLK),
            sample_weight,
            residual,
            variant_weight.reshape(local_blocks, BLK),
            block_gene.reshape(1, -1),
            gene_variants.reshape(1, -1),
        )
        return both[0], both[1]

    placed = (P("samp", "gene"), P("gene"), P(None, "samp"), P(None, "samp"), P("gene"), P(), P())
    return jax.shard_map(local, mesh=mesh, in_specs=placed, out_specs=(P(), P()), check_vma=False)
```

time: 16.1 us -> 16.2 us (level)
  no operation moved by 1% of the time
where the time goes in v4:
time: 16.2 us; the launch traced here: 16 us
  Pallas kernels  14.8 us (91%)
  between operations  0.64 us (4%)
  local copies, waits for them, and re-layouts  0.52 us (3%)
    pallas_call x1, Pallas kernels, local(): pl.pallas_call(functools.partial(kernel, samp_size, gene_size, owner_low,...  14.8 us
    squeeze x1, local copies, waits for them, and re-layouts, local(): return (both[0], both[1])  0.52 us

profile of v4, /device:TPU:0, one launch (start us, length us, event | category | flops | bytes accessed | tf_op | source)
XLA Modules:
  0.0 16.0 jit_solution(16136497856448245471)
XLA Ops:
  0.6 14.8 %shard_map.86 = f32[2,16]{1,0:T(2,128)S(1)} custom-call(s32[32,1024]{1,0:T(8,128)} %genotypes_hbm.1, f32[8,128]{1,0:T(8,128)} %bitcast.8, f32[16,32]{1,0:T(8,128)} %weight_hbm.1, f32[16,32]{1,0:T(8,128)} %residual_hbm.1, f32[8,128]{1,0:T(8,128)} %bitcast.9, s32[1,32]{1,0:T(1,128)} %bitcast.10, s32[1,16]{1,0:T(1,128)} %bitcast.11), custom_call_target="tpu_custom_call" | custom-call | tf_op jit(solution)/shard_map/pallas_call | solution.py:495
  15.5 0.5 %slice_bitcast_fusion = (f32[16]{0:T(128)}, f32[16]{0:T(128)}) fusion(f32[2,16]{1,0:T(2,128)S(1)} %shard_map.86), kind=kLoop, calls=%fused_computation | loop fusion | bytes 256 | tf_op jit(solution)/shard_map/squeeze | solution.py:535

commit v5 on v4

v5 whole, which is shorter than its diff:
```python
import functools

import jax
import jax.numpy as jnp
from jax import lax
from jax.experimental import pallas as pl
from jax.experimental.pallas import tpu as pltpu
from jax.sharding import PartitionSpec as P

BLK = 128
MESH = pl.DeviceIdType.MESH
STATS = 5
SCORE = 16
PAIR = 2
TURNS = (
    (1, (1,)),
    (0, (0, 1)),
    (1, (6, 7)),
    (1, (4, 5)),
    (0, (4, 5)),
    (1, (2, 3)),
    (0, (6, 7)),
    (0, (2, 3)),
)


def lane_sum(row):
    return jnp.sum(row, axis=1, keepdims=True)


def owner_range(samp_size, local_blocks):
    low = samp_size // 4
    size = max(1, samp_size // 2)
    while local_blocks % size:
        size -= 1
    return low, size


def flip(samp, step):
    peer, bit = samp, 1
    while bit <= step:
        if step & bit:
            peer = peer + bit * (1 - 2 * lax.rem(lax.div(samp, bit), 2))
        bit *= 2
    return peer


def kernel(
    samp_size,
    gene_size,
    owner_low,
    owner_size,
    genotypes_hbm,
    freq_hbm,
    weight_hbm,
    residual_hbm,
    variant_hbm,
    block_gene_hbm,
    counts_hbm,
    both_ref,
    words_in,
    weight_in,
    residual_in,
    block_gene_in,
    counts_in,
    params,
    tile_out,
    tiles,
    lead_words,
    given_words,
    centers,
    pair_weight,
    row_out,
    rows,
    load_sem,
    send_sem,
    tile_sem,
    lead_sem,
    given_sem,
    param_sem,
    row_sem,
    answer_sem,
    known_sem,
):
    samp = lax.axis_index("samp")
    gene = lax.axis_index("gene")
    side = lax.rem(gene, PAIR)
    lead = gene - side + (PAIR - 1)
    fields, local_rows = weight_in.shape
    group = BLK // local_rows
    depth = fields // group
    local_blocks = params.shape[2]
    owned = local_blocks // owner_size
    owner_high = owner_low + owner_size
    genes = counts_in.shape[1]
    width = row_out.shape[1]
    leads = side == PAIR - 1
    in_range = jnp.logical_and(samp >= owner_low, samp < owner_high)
    owns = jnp.logical_and(leads, in_range)
    helps = jnp.logical_and(jnp.logical_not(leads), in_range)
    place = samp - owner_low
    row_count = rows.shape[0]

    loads = [
        pltpu.make_async_copy(source, target, load_sem.at[number])
        for number, source, target in (
            (0, genotypes_hbm, words_in),
            (1, weight_hbm, weight_in),
            (1, residual_hbm, residual_in),
            (2, freq_hbm, params.at[side, 0]),
            (2, variant_hbm, params.at[side, 1]),
            (2, block_gene_hbm, block_gene_in),
            (2, counts_hbm, counts_in),
        )
    ]
    for load in loads[1:] + loads[:1]:
        load.start()

    def signal(semaphore, samp_to, gene_to):
        pl.semaphore_signal(
            semaphore,
            inc=1,
            device_id={"samp": samp_to, "gene": gene_to},
            device_id_type=MESH,
        )

    barrier = pltpu.get_barrier_semaphore()

    @pl.when(leads)
    def _():
        signal(barrier, samp, gene - 1)

    @pl.when(owns)
    def _():
        @pl.loop(1, samp_size)
        def _(step):
            for other in range(PAIR):
                signal(barrier, lax.rem(samp + step, samp_size), gene - other)

    for gene_to in range(PAIR, gene_size):

        @pl.when(gene_to > lead)
        def _(gene_to=gene_to):
            signal(barrier, samp, gene_to)

    loads[1].wait()
    loads[2].wait()
    own_tile = jnp.concatenate(
        [
            jnp.concatenate(
                [part[lanes * depth : (lanes + 1) * depth] for lanes in range(group)], axis=1
            )
            for part in (weight_in[...], residual_in[...])
        ],
        axis=0,
    )
    tile_out[...] = own_tile
    tiles[samp] = own_tile

    targets = jnp.where(in_range, owner_size - 1, owner_size)
    earlier = lead - (PAIR - 1)
    pl.semaphore_wait(barrier, jnp.where(leads, targets, targets + 1) + earlier)

    def tile_copy(owner):
        return pltpu.make_async_remote_copy(
            src_ref=tile_out,
            dst_ref=tiles.at[samp],
            send_sem=send_sem,
            recv_sem=tile_sem.at[lax.div(samp, 2)],
            device_id={"samp": owner, "gene": gene},
            device_id_type=MESH,
        )

    def word_copy(target, semaphore):
        def copy(owner):
            start = pl.multiple_of((owner - owner_low) * (owned * BLK), BLK)
            return pltpu.make_async_remote_copy(
                src_ref=words_in.at[:, pl.ds(start, owned * BLK)],
                dst_ref=target.at[samp],
                send_sem=send_sem,
                recv_sem=semaphore,
                device_id={"samp": owner, "gene": lead},
                device_id_type=MESH,
            )

        return copy

    upward = 2 * samp < 2 * owner_low + owner_size

    def to_owner(send, order, here=False):
        owner = jnp.where(upward, owner_high - 1 - order, owner_low + order)
        if here:
            send(owner).start()
        else:

            @pl.when(owner != samp)
            def _():
                send(owner).start()

    def to_owners(send, here=False):
        for order in range(owner_size):
            to_owner(send, order, here)

    @pl.when(leads)
    def _():
        to_owners(tile_copy)

    loads[0].wait()

    @pl.when(leads)
    def _():
        to_owners(word_copy(lead_words, lead_sem.at[lax.div(samp, 2)]))

    @pl.when(jnp.logical_not(leads))
    def _():
        to_owners(word_copy(given_words, given_sem.at[lax.div(samp, 2)]), True)

    for gene_to in range(gene_size - PAIR):

        @pl.when(gene_to < earlier)
        def _(gene_to=gene_to):
            signal(answer_sem, samp, gene_to)

    for load in loads[3:]:
        load.wait()
    later = gene_size - 1 - lead

    @pl.when(helps)
    def _():
        pltpu.make_async_remote_copy(
            src_ref=params.at[0],
            dst_ref=params.at[0],
            send_sem=send_sem,
            recv_sem=param_sem,
            device_id={"samp": samp, "gene": lead},
            device_id_type=MESH,
        ).start()

    @pl.when(later > 0)
    def _():
        pl.semaphore_wait(answer_sem, later)

        @pl.loop(owner_low, owner_high)
        def _(owner):
            @pl.when(jnp.logical_and(owner != samp, leads))
            def _():
                signal(known_sem, owner, gene)

    @pl.when(owns)
    def _():
        pltpu.make_async_copy(params.at[0], params.at[0], param_sem).wait()
        block_gene = block_gene_in[...].astype(jnp.float32)
        counts = counts_in[...].astype(jnp.float32)
        block_lane = lax.broadcasted_iota(jnp.int32, block_gene.shape, 1)
        gene_lane = lax.broadcasted_iota(jnp.int32, counts.shape, 1).astype(jnp.float32)
        column = lax.broadcasted_iota(jnp.int32, (1, BLK), 1).astype(jnp.float32)
        stat_sub = lax.broadcasted_iota(jnp.int32, (8, width), 0)
        stat_lane = lax.broadcasted_iota(jnp.int32, (8, width), 1) - stat_sub * genes
        effective, places = [], []
        for number in range(PAIR * owned):
            from_side, block = divmod(number, owned)
            local_block = place * owned + block
            block_id = (lead - (PAIR - 1) + from_side) * local_blocks + local_block
            gene_of = lane_sum(jnp.where(block_lane == block_id, block_gene, 0.0))
            first = lane_sum(jnp.where(block_gene < gene_of, 1.0, 0.0))
            counted = lane_sum(jnp.where(gene_lane == gene_of, counts, 0.0))
            block_float = jnp.zeros((1, 1), jnp.float32) + block_id.astype(jnp.float32)
            live = (block_float - first) * BLK + column < counted
            weights = jnp.where(live, params[from_side, 1, pl.ds(local_block, 1), :], 0.0)
            effective.append(weights)
            across = jnp.broadcast_to(weights, (BLK, BLK))
            pair_weight[number] = across * across.T
            freq = params[from_side, 0, pl.ds(local_block, 1), :]
            center = 2.0 * jnp.broadcast_to(freq, (BLK, BLK)).T
            for level in range(depth):
                centers[number, level] = center * float(4**level)
            member = stat_lane.astype(jnp.float32) == gene_of
            places.append(jnp.where(member & (stat_sub < STATS), 1.0, 0.0))

        def land(buffer, semaphore):
            pltpu.make_async_copy(buffer, buffer, semaphore).wait()

        def unpack(from_side, peer, power):
            tile = tiles[peer]
            weight, resid = tile[:depth], tile[depth:]
            root = jnp.sqrt(weight)
            score = root * resid
            if from_side:
                power = power + weight * resid * resid
            values = []
            buffer = lead_words if from_side else given_words
            for block in range(owned):
                part = buffer[peer, :, block * BLK : (block + 1) * BLK]
                turned = jnp.concatenate(
                    [lax.shift_right_logical(part, 2 * depth * lanes) for lanes in range(group)],
                    axis=0,
                ).T
                levels = []
                for level in range(depth):
                    dosage = jnp.bitwise_and(turned, 3 << (2 * level)).astype(jnp.float32)
                    scale = root[level : level + 1] * float(4**-level)
                    center = centers[from_side * owned + block, level]
                    levels.append(((dosage - center) * scale).astype(jnp.bfloat16))
                values.append(jnp.concatenate(levels, axis=1))
            scores = jnp.concatenate(
                [
                    jnp.broadcast_to(score[level : level + 1], (SCORE, BLK)).astype(jnp.bfloat16)
                    for level in range(depth)
                ],
                axis=1,
            )
            return (from_side, values, scores), power

        def multiply(unpacked, totals):
            from_side, values, scores = unpacked
            totals = list(totals)
            for block in range(owned):
                number = from_side * owned + block
                totals[number] = totals[number] + lax.dot_general(
                    jnp.concatenate([values[block], scores], axis=0),
                    values[block],
                    (((1,), (1,)), ((), ())),
                    preferred_element_type=jnp.float32,
                )
            return tuple(totals)

        own_start = pl.multiple_of(place * (owned * BLK), BLK)
        lead_words[samp] = words_in[:, pl.ds(own_start, owned * BLK)]

        diagonal = lax.broadcasted_iota(jnp.int32, (BLK, BLK), 0) == lax.broadcasted_iota(
            jnp.int32, (BLK, BLK), 1
        )

        def finish(from_side, totals, message):
            for block in range(owned):
                number = from_side * owned + block
                total = totals[number]
                weighted = total[:BLK] * pair_weight[number]
                score = effective[number] * total[BLK : BLK + 1]
                sums = [
                    score,
                    jnp.sum(weighted, axis=0, keepdims=True),
                    score * score,
                    jnp.sum(jnp.where(diagonal, weighted, 0.0), axis=0, keepdims=True),
                    jnp.sum(weighted * weighted, axis=0, keepdims=True),
                    jnp.zeros((8 - STATS, BLK), jnp.float32),
                ]
                message = message + lane_sum(jnp.concatenate(sums, axis=0)) * places[number]
            return message

        def land_lead(first, count):
            two = lax.div(first, 2)
            land(tiles.at[pl.ds(first, count)], tile_sem.at[two])
            land(lead_words.at[pl.ds(first, count)], lead_sem.at[two])

        def land_given(first):
            land(given_words.at[pl.ds(first, 2)], given_sem.at[lax.div(first, 2)])

        message = jnp.zeros((8, width), jnp.float32)
        power = jnp.zeros((depth, BLK), jnp.float32)
        totals = tuple(jnp.zeros((BLK + SCORE, BLK), jnp.float32) for _ in range(PAIR * owned))
        if samp_size == 8:
            waiting, power = unpack(PAIR - 1, samp, power)
            for number, (from_side, steps) in enumerate(TURNS):
                peers = [flip(samp, step) for step in steps]
                pair = samp - lax.rem(samp, 2)
                if steps[0] > 1:
                    pair = flip(pair, steps[0])
                if from_side == 0:
                    land_given(pair)
                elif len(steps) == 1:
                    land_lead(peers[0], 1)
                else:
                    land_lead(pair, 2)
                for peer in peers:
                    ahead, power = unpack(from_side, peer, power)
                    totals = multiply(waiting, totals)
                    waiting = ahead
                if all(side == 0 for side, _ in TURNS[number:]) and TURNS[number - 1][0]:
                    message = finish(PAIR - 1, totals, message)
            totals = multiply(waiting, totals)
            message = finish(0, totals, message)
        else:
            ahead, power = unpack(PAIR - 1, samp, power)
            totals = multiply(ahead, totals)
            partner = samp + 1 - 2 * lax.rem(samp, 2)
            land_lead(partner, 1)
            ahead, power = unpack(PAIR - 1, partner, power)
            totals = multiply(ahead, totals)

            def add_lead(step, carry):
                totals, power = carry
                first = 2 * lax.rem(lax.div(samp, 2) + step, samp_size // 2)
                land_lead(first, 2)
                for member in range(2):
                    ahead, power = unpack(PAIR - 1, first + member, power)
                    totals = multiply(ahead, totals)
                return totals, power

            def add_given(two, totals):
                land_given(two * 2)
                for member in range(2):
                    totals = multiply(unpack(0, two * 2 + member, power)[0], totals)
                return totals

            totals, power = lax.fori_loop(1, samp_size // 2, add_lead, (totals, power))
            totals = lax.fori_loop(0, samp_size // 2, add_given, totals)
            for from_side in range(PAIR):
                message = finish(from_side, totals, message)
        squares = lane_sum(jnp.sum(power, axis=0, keepdims=True))
        reports = jnp.logical_and(place == 0, gene == PAIR - 1).astype(jnp.float32)
        lane = lax.broadcasted_iota(jnp.int32, (8, width), 1)
        message = message + jnp.where(
            (lane == STATS * genes) & (stat_sub == 0), squares * reports, 0.0
        )
        row = jnp.sum(message, axis=0, keepdims=True)

        @pl.when(later > 0)
        def _():
            pl.semaphore_wait(known_sem, samp_size - 1)

        row_out[...] = row
        slot = place * (gene_size // PAIR) + lax.div(gene, PAIR)
        rows[slot] = row

        @pl.loop(0, samp_size)
        def _(samp_to):
            for gene_to in range(gene_size):

                @pl.when(jnp.logical_or(samp_to != samp, gene_to != gene))
                def _(gene_to=gene_to):
                    pltpu.make_async_remote_copy(
                        src_ref=row_out,
                        dst_ref=rows.at[slot],
                        send_sem=send_sem,
                        recv_sem=row_sem,
                        device_id={"samp": samp_to, "gene": gene_to},
                        device_id_type=MESH,
                    ).start()

    @pl.when(owns)
    def _():
        landed = rows.at[pl.ds(0, row_count - 1)]
        pltpu.make_async_copy(landed, landed, row_sem).wait()

    @pl.when(jnp.logical_not(owns))
    def _():
        pltpu.make_async_copy(rows, rows, row_sem).wait()

    totals = jnp.sum(rows[...], axis=0)
    parts = [totals[:, stat * genes : (stat + 1) * genes] for stat in range(STATS)]
    variance = totals[:, STATS * genes : STATS * genes + 1] / (fields * local_rows * samp_size)
    both_ref[0:1] = parts[0] / jnp.sqrt(variance * parts[1])
    both_ref[1:2] = (parts[2] - variance * parts[3]) / (
        variance * jnp.sqrt(2.0 * parts[4])
    )

    def sent(buffer, count):
        @pl.loop(0, count)
        def _(_):
            pltpu.make_async_copy(buffer, buffer, send_sem).wait()

    sent(tile_out, jnp.where(leads, targets, 0))
    sent(lead_words.at[0], jnp.where(leads, targets, owner_size))
    sent(params.at[0], jnp.where(helps, 1, 0))
    sent(row_out, jnp.where(owns, samp_size * gene_size - 1, 0))


def solution(mesh):
    samp_size, gene_size = mesh.shape["samp"], mesh.shape["gene"]

    def local(
        genotypes, allele_freq, sample_weight, residual, variant_weight, block_gene, gene_variants
    ):
        local_rows, columns = genotypes.shape
        local_blocks = columns // BLK
        fields = sample_weight.shape[0]
        genes = gene_variants.shape[0]
        depth = fields * local_rows // BLK
        width = -(-(STATS * genes + 1) // BLK) * BLK
        owner_low, owner_size = owner_range(samp_size, local_blocks)
        owned = local_blocks // owner_size
        both = pl.pallas_call(
            functools.partial(kernel, samp_size, gene_size, owner_low, owner_size),
            out_shape=pltpu.VMEM((2, genes), jnp.float32),
            in_specs=[pl.BlockSpec(memory_space=pl.ANY)] * 7,
            out_specs=pl.BlockSpec(memory_space=pltpu.VMEM),
            scratch_shapes=[
                pltpu.VMEM((local_rows, columns), jnp.int32),
                pltpu.VMEM((fields, local_rows), jnp.float32),
                pltpu.VMEM((fields, local_rows), jnp.float32),
                pltpu.VMEM((1, block_gene.shape[0]), jnp.int32),
                pltpu.VMEM((1, genes), jnp.int32),
                pltpu.VMEM((PAIR, 2, local_blocks, BLK), jnp.float32),
                pltpu.VMEM((2 * depth, BLK), jnp.float32),
                pltpu.VMEM((samp_size, 2 * depth, BLK), jnp.float32),
                pltpu.VMEM((samp_size, local_rows, owned * BLK), jnp.int32),
                pltpu.VMEM((samp_size, local_rows, owned * BLK), jnp.int32),
                pltpu.VMEM((PAIR * owned, depth, BLK, BLK), jnp.float32),
                pltpu.VMEM((PAIR * owned, BLK, BLK), jnp.float32),
                pltpu.VMEM((1, width), jnp.float32),
                pltpu.VMEM((owner_size * gene_size // PAIR, 1, width), jnp.float32),
                pltpu.SemaphoreType.DMA((3,)),
                pltpu.SemaphoreType.DMA,
                pltpu.SemaphoreType.DMA((samp_size // 2,)),
                pltpu.SemaphoreType.DMA((samp_size // 2,)),
                pltpu.SemaphoreType.DMA((samp_size // 2,)),
                pltpu.SemaphoreType.DMA,
                pltpu.SemaphoreType.DMA,
                pltpu.SemaphoreType.REGULAR,
                pltpu.SemaphoreType.REGULAR,
            ],
            compiler_params=pltpu.CompilerParams(collective_id=0, has_side_effects=True),
        )(
            genotypes,
            allele_freq.reshape(local_blocks, BLK),
            sample_weight,
            residual,
            variant_weight.reshape(local_blocks, BLK),
            block_gene.reshape(1, -1),
            gene_variants.reshape(1, -1),
        )
        return both[0], both[1]

    placed = (P("samp", "gene"), P("gene"), P(None, "samp"), P(None, "samp"), P("gene"), P(), P())
    return jax.shard_map(local, mesh=mesh, in_specs=placed, out_specs=(P(), P()), check_vma=False)
```

time: 16.2 us -> 15.7 us (0.969)
  Pallas kernels: 14.8 us -> 14.4 us
    pallas_call x1, Pallas kernels: 14.8 us -> 14.4 us  [local(): pl.pallas_call(functools.partial(kernel, samp_size, gene_size, owner_low,...]
where the time goes in v5:
time: 15.7 us; the launch traced here: 15.5 us
  Pallas kernels  14.4 us (92%)
  between operations  0.64 us (4%)
  local copies, waits for them, and re-layouts  0.52 us (3%)
    pallas_call x1, Pallas kernels, local(): pl.pallas_call(functools.partial(kernel, samp_size, gene_size, owner_low,...  14.4 us
    squeeze x1, local copies, waits for them, and re-layouts, local(): return (both[0], both[1])  0.52 us

profile of v5, /device:TPU:0, one launch (start us, length us, event | category | flops | bytes accessed | tf_op | source)
XLA Modules:
  0.0 15.5 jit_solution(12649311860417220577)
XLA Ops:
  0.6 14.4 %shard_map.86 = f32[2,16]{1,0:T(2,128)S(1)} custom-call(s32[32,1024]{1,0:T(8,128)} %genotypes_hbm.1, f32[8,128]{1,0:T(8,128)} %bitcast.8, f32[16,32]{1,0:T(8,128)} %weight_hbm.1, f32[16,32]{1,0:T(8,128)} %residual_hbm.1, f32[8,128]{1,0:T(8,128)} %bitcast.9, s32[1,32]{1,0:T(1,128)} %bitcast.10, s32[1,16]{1,0:T(1,128)} %bitcast.11), custom_call_target="tpu_custom_call" | custom-call | tf_op jit(solution)/shard_map/pallas_call | solution.py:483
  15.0 0.5 %slice_bitcast_fusion = (f32[16]{0:T(128)}, f32[16]{0:T(128)}) fusion(f32[2,16]{1,0:T(2,128)S(1)} %shard_map.86), kind=kLoop, calls=%fused_computation | loop fusion | bytes 256 | tf_op jit(solution)/shard_map/squeeze | solution.py:523

commit v6 on v5

--- a/solution.py
+++ b/solution.py
@@ -107,13 +107,13 @@
             (0, genotypes_hbm, words_in),
             (1, weight_hbm, weight_in),
             (1, residual_hbm, residual_in),
-            (2, freq_hbm, params.at[side, 0]),
-            (2, variant_hbm, params.at[side, 1]),
-            (2, block_gene_hbm, block_gene_in),
-            (2, counts_hbm, counts_in),
+            (1, freq_hbm, params.at[side, 0]),
+            (1, variant_hbm, params.at[side, 1]),
+            (1, block_gene_hbm, block_gene_in),
+            (1, counts_hbm, counts_in),
         )
     ]
-    for load in loads[1:] + loads[:1]:
+    for load in loads:
         load.start()
 
     def signal(semaphore, samp_to, gene_to):
@@ -143,8 +143,8 @@
         def _(gene_to=gene_to):
             signal(barrier, samp, gene_to)
 
-    loads[1].wait()
-    loads[2].wait()
+    for load in loads[1:]:
+        load.wait()
     own_tile = jnp.concatenate(
         [
             jnp.concatenate(
@@ -221,8 +221,6 @@
         def _(gene_to=gene_to):
             signal(answer_sem, samp, gene_to)
 
-    for load in loads[3:]:
-        load.wait()
     later = gene_size - 1 - lead
 
     @pl.when(helps)
@@ -409,9 +407,8 @@
                 message = finish(from_side, totals, message)
         squares = lane_sum(jnp.sum(power, axis=0, keepdims=True))
         reports = jnp.logical_and(place == 0, gene == PAIR - 1).astype(jnp.float32)
-        lane = lax.broadcasted_iota(jnp.int32, (8, width), 1)
         message = message + jnp.where(
-            (lane == STATS * genes) & (stat_sub == 0), squares * reports, 0.0
+            (stat_sub == STATS) & (stat_lane >= 0) & (stat_lane < genes), squares * reports, 0.0
         )
         row = jnp.sum(message, axis=0, keepdims=True)
 
@@ -448,12 +445,10 @@
         pltpu.make_async_copy(rows, rows, row_sem).wait()
 
     totals = jnp.sum(rows[...], axis=0)
-    parts = [totals[:, stat * genes : (stat + 1) * genes] for stat in range(STATS)]
-    variance = totals[:, STATS * genes : STATS * genes + 1] / (fields * local_rows * samp_size)
-    both_ref[0:1] = parts[0] / jnp.sqrt(variance * parts[1])
-    both_ref[1:2] = (parts[2] - variance * parts[3]) / (
-        variance * jnp.sqrt(2.0 * parts[4])
-    )
+    parts = [totals[:, stat * genes : (stat + 1) * genes] for stat in range(STATS + 1)]
+    variance = parts[STATS] / (fields * local_rows * samp_size)
+    both_ref[0:1] = parts[0] * lax.rsqrt(variance * parts[1])
+    both_ref[1:2] = (parts[2] - variance * parts[3]) * lax.rsqrt(2.0 * parts[4]) / variance
 
     def sent(buffer, count):
         @pl.loop(0, count)
@@ -477,7 +472,7 @@
         fields = sample_weight.shape[0]
         genes = gene_variants.shape[0]
         depth = fields * local_rows // BLK
-        width = -(-(STATS * genes + 1) // BLK) * BLK
+        width = -(-((STATS + 1) * genes) // BLK) * BLK
         owner_low, owner_size = owner_range(samp_size, local_blocks)
         owned = local_blocks // owner_size
         both = pl.pallas_call(
@@ -500,7 +495,7 @@
                 pltpu.VMEM((PAIR * owned, BLK, BLK), jnp.float32),
                 pltpu.VMEM((1, width), jnp.float32),
                 pltpu.VMEM((owner_size * gene_size // PAIR, 1, width), jnp.float32),
-                pltpu.SemaphoreType.DMA((3,)),
+                pltpu.SemaphoreType.DMA((2,)),
                 pltpu.SemaphoreType.DMA,
                 pltpu.SemaphoreType.DMA((samp_size // 2,)),
                 pltpu.SemaphoreType.DMA((samp_size // 2,)),

time: 15.7 us -> 15.6 us (level)
  no operation moved by 1% of the time
where the time goes in v6:
time: 15.6 us; the launch traced here: 15.4 us
  Pallas kernels  14.3 us (92%)
  between operations  0.64 us (4%)
  local copies, waits for them, and re-layouts  0.52 us (3%)
    pallas_call x1, Pallas kernels, local(): pl.pallas_call(functools.partial(kernel, samp_size, gene_size, owner_low,...  14.3 us
    squeeze x1, local copies, waits for them, and re-layouts, local(): return (both[0], both[1])  0.52 us

profile of v6, /device:TPU:0, one launch (start us, length us, event | category | flops | bytes accessed | tf_op | source)
XLA Modules:
  0.0 15.4 jit_solution(878429781256030340)
XLA Ops:
  0.6 14.3 %shard_map.86 = f32[2,16]{1,0:T(2,128)S(1)} custom-call(s32[32,1024]{1,0:T(8,128)} %genotypes_hbm.1, f32[8,128]{1,0:T(8,128)} %bitcast.8, f32[16,32]{1,0:T(8,128)} %weight_hbm.1, f32[16,32]{1,0:T(8,128)} %residual_hbm.1, f32[8,128]{1,0:T(8,128)} %bitcast.9, s32[1,32]{1,0:T(1,128)} %bitcast.10, s32[1,16]{1,0:T(1,128)} %bitcast.11), custom_call_target="tpu_custom_call" | custom-call | tf_op jit(solution)/shard_map/pallas_call | solution.py:478
  14.9 0.5 %slice_bitcast_fusion = (f32[16]{0:T(128)}, f32[16]{0:T(128)}) fusion(f32[2,16]{1,0:T(2,128)S(1)} %shard_map.86), kind=kLoop, calls=%fused_computation | loop fusion | bytes 256 | tf_op jit(solution)/shard_map/squeeze | solution.py:518

commit v7 on v6

--- a/solution.py
+++ b/solution.py
@@ -15,8 +15,8 @@
 TURNS = (
     (1, (1,)),
     (0, (0, 1)),
+    (1, (4, 5)),
     (1, (6, 7)),
-    (1, (4, 5)),
     (0, (4, 5)),
     (1, (2, 3)),
     (0, (6, 7)),
@@ -278,7 +278,7 @@
         def land(buffer, semaphore):
             pltpu.make_async_copy(buffer, buffer, semaphore).wait()
 
-        def unpack(from_side, peer, power):
+        def unpack(from_side, peer, power, blocks=tuple(range(owned))):
             tile = tiles[peer]
             weight, resid = tile[:depth], tile[depth:]
             root = jnp.sqrt(weight)
@@ -287,7 +287,7 @@
                 power = power + weight * resid * resid
             values = []
             buffer = lead_words if from_side else given_words
-            for block in range(owned):
+            for block in blocks:
                 part = buffer[peer, :, block * BLK : (block + 1) * BLK]
                 turned = jnp.concatenate(
                     [lax.shift_right_logical(part, 2 * depth * lanes) for lanes in range(group)],
@@ -307,16 +307,16 @@
                 ],
                 axis=1,
             )
-            return (from_side, values, scores), power
+            return (from_side, blocks, values, scores), power
 
         def multiply(unpacked, totals):
-            from_side, values, scores = unpacked
+            from_side, blocks, values, scores = unpacked
             totals = list(totals)
-            for block in range(owned):
+            for value, block in zip(values, blocks):
                 number = from_side * owned + block
                 totals[number] = totals[number] + lax.dot_general(
-                    jnp.concatenate([values[block], scores], axis=0),
-                    values[block],
+                    jnp.concatenate([value, scores], axis=0),
+                    value,
                     (((1,), (1,)), ((), ())),
                     preferred_element_type=jnp.float32,
                 )
@@ -370,12 +370,19 @@
                     land_lead(peers[0], 1)
                 else:
                     land_lead(pair, 2)
+                if number == len(TURNS) - 1:
+                    message = finish(PAIR - 1, totals, message)
+                if number == len(TURNS) - 1:
+                    for block in range(owned):
+                        for peer in peers:
+                            ahead, power = unpack(from_side, peer, power, (block,))
+                            totals = multiply(waiting, totals)
+                            waiting = ahead
+                    continue
                 for peer in peers:
                     ahead, power = unpack(from_side, peer, power)
                     totals = multiply(waiting, totals)
                     waiting = ahead
-                if all(side == 0 for side, _ in TURNS[number:]) and TURNS[number - 1][0]:
-                    message = finish(PAIR - 1, totals, message)
             totals = multiply(waiting, totals)
             message = finish(0, totals, message)
         else:

time: 15.6 us -> 15.5 us (level)
  no operation moved by 1% of the time
where the time goes in v7:
time: 15.5 us; the launch traced here: 15.3 us
  Pallas kernels  14.2 us (92%)
  between operations  0.64 us (4%)
  local copies, waits for them, and re-layouts  0.52 us (3%)
    pallas_call x1, Pallas kernels, local(): pl.pallas_call(functools.partial(kernel, samp_size, gene_size, owner_low,...  14.2 us
    squeeze x1, local copies, waits for them, and re-layouts, local(): return (both[0], both[1])  0.52 us

profile of v7, /device:TPU:0, one launch (start us, length us, event | category | flops | bytes accessed | tf_op | source)
XLA Modules:
  0.0 15.3 jit_solution(9615895598872944153)
XLA Ops:
  0.6 14.2 %shard_map.86 = f32[2,16]{1,0:T(2,128)S(1)} custom-call(s32[32,1024]{1,0:T(8,128)} %genotypes_hbm.1, f32[8,128]{1,0:T(8,128)} %bitcast.8, f32[16,32]{1,0:T(8,128)} %weight_hbm.1, f32[16,32]{1,0:T(8,128)} %residual_hbm.1, f32[8,128]{1,0:T(8,128)} %bitcast.9, s32[1,32]{1,0:T(1,128)} %bitcast.10, s32[1,16]{1,0:T(1,128)} %bitcast.11), custom_call_target="tpu_custom_call" | custom-call | tf_op jit(solution)/shard_map/pallas_call | solution.py:485
  14.8 0.5 %slice_bitcast_fusion = (f32[16]{0:T(128)}, f32[16]{0:T(128)}) fusion(f32[2,16]{1,0:T(2,128)S(1)} %shard_map.86), kind=kLoop, calls=%fused_computation | loop fusion | bytes 256 | tf_op jit(solution)/shard_map/squeeze | solution.py:525

commit v8 on v7

--- a/solution.py
+++ b/solution.py
@@ -15,10 +15,13 @@
 TURNS = (
     (1, (1,)),
     (0, (0, 1)),
-    (1, (4, 5)),
-    (1, (6, 7)),
+    (1, (6,)),
+    (1, (4,)),
+    (1, (7,)),
+    (1, (5,)),
+    (1, (2,)),
     (0, (4, 5)),
-    (1, (2, 3)),
+    (1, (3,)),
     (0, (6, 7)),
     (0, (2, 3)),
 )
@@ -209,7 +212,7 @@
 
     @pl.when(leads)
     def _():
-        to_owners(word_copy(lead_words, lead_sem.at[lax.div(samp, 2)]))
+        to_owners(word_copy(lead_words, lead_sem.at[samp]))
 
     @pl.when(jnp.logical_not(leads))
     def _():
@@ -346,10 +349,11 @@
                 message = message + lane_sum(jnp.concatenate(sums, axis=0)) * places[number]
             return message
 
-        def land_lead(first, count):
-            two = lax.div(first, 2)
-            land(tiles.at[pl.ds(first, count)], tile_sem.at[two])
-            land(lead_words.at[pl.ds(first, count)], lead_sem.at[two])
+        def land_tiles(first, count):
+            land(tiles.at[pl.ds(first, count)], tile_sem.at[lax.div(first, 2)])
+
+        def land_lead(peer):
+            land(lead_words.at[peer], lead_sem.at[peer])
 
         def land_given(first):
             land(given_words.at[pl.ds(first, 2)], given_sem.at[lax.div(first, 2)])
@@ -363,13 +367,16 @@
                 peers = [flip(samp, step) for step in steps]
                 pair = samp - lax.rem(samp, 2)
                 if steps[0] > 1:
-                    pair = flip(pair, steps[0])
+                    pair = flip(pair, steps[0] - steps[0] % 2)
                 if from_side == 0:
                     land_given(pair)
-                elif len(steps) == 1:
-                    land_lead(peers[0], 1)
                 else:
-                    land_lead(pair, 2)
+                    if steps[0] == 1:
+                        land_tiles(peers[0], 1)
+                    elif steps[0] % 2 == 0:
+                        land_tiles(pair, 2)
+                    for peer in peers:
+                        land_lead(peer)
                 if number == len(TURNS) - 1:
                     message = finish(PAIR - 1, totals, message)
                 if number == len(TURNS) - 1:
@@ -389,14 +396,17 @@
             ahead, power = unpack(PAIR - 1, samp, power)
             totals = multiply(ahead, totals)
             partner = samp + 1 - 2 * lax.rem(samp, 2)
-            land_lead(partner, 1)
+            land_tiles(partner, 1)
+            land_lead(partner)
             ahead, power = unpack(PAIR - 1, partner, power)
             totals = multiply(ahead, totals)
 
             def add_lead(step, carry):
                 totals, power = carry
                 first = 2 * lax.rem(lax.div(samp, 2) + step, samp_size // 2)
-                land_lead(first, 2)
+                land_tiles(first, 2)
+                land_lead(first)
+                land_lead(first + 1)
                 for member in range(2):
                     ahead, power = unpack(PAIR - 1, first + member, power)
                     totals = multiply(ahead, totals)
@@ -505,7 +515,7 @@
                 pltpu.SemaphoreType.DMA((2,)),
                 pltpu.SemaphoreType.DMA,
                 pltpu.SemaphoreType.DMA((samp_size // 2,)),
-                pltpu.SemaphoreType.DMA((samp_size // 2,)),
+                pltpu.SemaphoreType.DMA((samp_size,)),
                 pltpu.SemaphoreType.DMA((samp_size // 2,)),
                 pltpu.SemaphoreType.DMA,
                 pltpu.SemaphoreType.DMA,

time: 15.5 us -> 15.4 us (level)
  no operation moved by 1% of the time
where the time goes in v8:
time: 15.4 us; the launch traced here: 15.2 us
  Pallas kernels  14.1 us (92%)
  between operations  0.64 us (4%)
  local copies, waits for them, and re-layouts  0.52 us (3%)
    pallas_call x1, Pallas kernels, local(): pl.pallas_call(functools.partial(kernel, samp_size, gene_size, owner_low,...  14.1 us
    squeeze x1, local copies, waits for them, and re-layouts, local(): return (both[0], both[1])  0.52 us

profile of v8, /device:TPU:0, one launch (start us, length us, event | category | flops | bytes accessed | tf_op | source)
XLA Modules:
  0.0 15.2 jit_solution(389055738228495107)
XLA Ops:
  0.6 14.1 %shard_map.86 = f32[2,16]{1,0:T(2,128)S(1)} custom-call(s32[32,1024]{1,0:T(8,128)} %genotypes_hbm.1, f32[8,128]{1,0:T(8,128)} %bitcast.8, f32[16,32]{1,0:T(8,128)} %weight_hbm.1, f32[16,32]{1,0:T(8,128)} %residual_hbm.1, f32[8,128]{1,0:T(8,128)} %bitcast.9, s32[1,32]{1,0:T(1,128)} %bitcast.10, s32[1,16]{1,0:T(1,128)} %bitcast.11), custom_call_target="tpu_custom_call" | custom-call | tf_op jit(solution)/shard_map/pallas_call | solution.py:495
  14.7 0.5 %slice_bitcast_fusion = (f32[16]{0:T(128)}, f32[16]{0:T(128)}) fusion(f32[2,16]{1,0:T(2,128)S(1)} %shard_map.86), kind=kLoop, calls=%fused_computation | loop fusion | bytes 256 | tf_op jit(solution)/shard_map/squeeze | solution.py:535
